TPU v7x, 128 devices: a 2x2x16 block of a 8x8x16 slice. The times are simulated.
128 devices in a mesh: group: 4 (over x, y), blk: 32 (over z, core).
Axes of the slice: x: 2, y: 2, z: 16, core: 2. Of those that a mesh axis runs over, the one named last changes fastest.
The devices are a block of a 8x8x16 slice.
Arguments:
- depth_logits: float32 [128, 112, 32, 128], P(('group', 'blk')), parts along dimension 0, may hold values from -18 to 300
- context: bfloat16 [128, 80, 32, 128], P(('group', 'blk')), parts along dimension 0, may hold values from -6 to 6
- lidar_bins: int32 [128, 32, 128], P(('group', 'blk')), parts along dimension 0, may hold values from -1 to 111, as said below
- az_map: int32 [8, 128], replicated, may hold values from 0 to 255, as said below
- rng_map: int32 [8, 112], replicated, may hold values from 0 to 511, as said below
- conv1_weight: bfloat16 [3, 3, 80, 256], replicated, may hold values from -0.21875 to 0.21875
- conv2_weight: bfloat16 [3, 3, 256, 256], replicated, may hold values from -0.125 to 0.125
- out_grad: bfloat16 [1024, 512, 256], P(('group', 'blk')), parts along dimension 0, may hold values from -6 to 6
Outputs:
- logit_grad: float32 [128, 112, 32, 128], P(('group', 'blk')), parts along dimension 0
- context_grad: bfloat16 [128, 80, 32, 128], P(('group', 'blk')), parts along dimension 0
- conv1_grad: float32 [12, 3, 80, 256], P('group'), parts along dimension 0
- conv2_grad: float32 [12, 3, 256, 256], P('group'), parts along dimension 0
There are 4 independent parts, one for each index of `group`. A program takes and returns all parts, laid end to end along the dimension named above; an argument that names none is the same for every part. Nothing has to cross between parts.
Inputs may be any that keep to these rules, and one draw needn't show every extreme that they name: `lidar_bins`: -1 marks a pixel without a LiDAR return. `az_map`: with S = 32, the columns of camera c, in order and never going back, run through the azimuth cells (c * S - S // 4 + t) mod 256 for t = 0 to 3 * S // 2 - 1, each such cell taking two or three columns. `rng_map`: for each camera the range cell rises strictly with the depth bin.
All inputs are finite; a program needn't handle non-finite values.
Results may differ from a plain program's by a relative error of at most 0.024.
Values may be sent and summed in bfloat16 or wider, within the bound.
A program may use at most 128 MiB of HBM per device.

v0:
```python
import jax
import jax.numpy as jnp
from jax import lax
from jax.experimental import pallas as pl
from jax.experimental.pallas import tpu as pltpu
from jax.sharding import PartitionSpec as P

DEPTH_WEIGHT = 3.0


def with_halo(cells, width):
    count = lax.axis_size("blk")
    head = cells[:width]
    tail = cells[cells.shape[0] - width :]
    return jnp.concatenate(
        [
            lax.ppermute(tail, "blk", [(i, (i + 1) % count) for i in range(count)]),
            cells,
            lax.ppermute(head, "blk", [((i + 1) % count, i) for i in range(count)]),
        ],
        axis=0,
    )


def silu_slope(value):
    logistic = jax.nn.sigmoid(value)
    return logistic * (1.0 + value * (1.0 - logistic))


def remote(src, dst, send_sem, recv_sem, target):
    return pltpu.make_async_remote_copy(
        src_ref=src,
        dst_ref=dst,
        send_sem=send_sem,
        recv_sem=recv_sem,
        device_id={"blk": target},
        device_id_type=pl.DeviceIdType.MESH,
    )


def greet(semaphore, target):
    pl.semaphore_signal(
        semaphore,
        inc=1,
        device_id={"blk": target},
        device_id_type=pl.DeviceIdType.MESH,
    )


def scatter_kernel(blocks, bands, pieces, sums, slots, send_sems, recv_sems):
    me = lax.axis_index("blk")
    band = me % bands
    first = me - band
    before = (first + blocks - bands) % blocks
    after = (first + bands) % blocks
    barrier = pltpu.get_barrier_semaphore()
    for other in range(bands):
        @pl.when(band != other)
        def _():
            greet(barrier, first + other)

        @pl.when(band == 0)
        def _():
            greet(barrier, before + other)

        @pl.when(band == bands - 1)
        def _():
            greet(barrier, after + other)
    pl.semaphore_wait(barrier, bands + 1)

    def outgoing(part):
        near = 1 <= part <= bands
        slot = band if near else bands + band
        target = (first + blocks - 1 + part) % blocks
        return remote(
            pieces.at[part], slots.at[slot], send_sems.at[part], recv_sems.at[slot], target
        )

    def arriving(slot):
        return remote(pieces.at[0], slots.at[slot], send_sems.at[0], recv_sems.at[slot], first)

    for part in (0, bands + 1):
        outgoing(part).start()
    for part in range(1, bands + 1):
        @pl.when(band != part - 1)
        def _():
            outgoing(part).start()
    slots[pl.ds(band, 1)] = pieces[pl.ds(band + 1, 1)]
    for slot in range(bands):
        @pl.when(band != slot)
        def _():
            arriving(slot).wait_recv()
    total = slots[0].astype(jnp.float32)
    for slot in range(1, bands):
        total = total + slots[slot].astype(jnp.float32)
    sums[0] = total.astype(sums.dtype)
    edge = jnp.logical_or(band == 0, band == bands - 1)

    @pl.when(edge)
    def _():
        for slot in range(bands, 2 * bands):
            arriving(slot).wait_recv()
        side = slots[bands].astype(jnp.float32)
        for slot in range(bands + 1, 2 * bands):
            side = side + slots[slot].astype(jnp.float32)
        sums[1] = side.astype(sums.dtype)

    @pl.when(jnp.logical_not(edge))
    def _():
        sums[1] = jnp.zeros(sums.shape[1:], sums.dtype)

    for part in (0, bands + 1):
        outgoing(part).wait_send()
    for part in range(1, bands + 1):
        @pl.when(band != part - 1)
        def _():
            outgoing(part).wait_send()


def reply_kernel(blocks, bands, replies, gathered, send_sems, recv_sems):
    me = lax.axis_index("blk")
    band = me % bands
    first = me - band
    before = (first + blocks - bands) % blocks
    after = (first + bands) % blocks
    edge = jnp.logical_or(band == 0, band == bands - 1)
    barrier = pltpu.get_barrier_semaphore()
    greet(barrier, (first + blocks - 1) % blocks)
    greet(barrier, after)
    for other in range(bands):
        @pl.when(band != other)
        def _():
            greet(barrier, first + other)

    @pl.when(edge)
    def _():
        pl.semaphore_wait(barrier, 2 * bands - 1)

    @pl.when(jnp.logical_not(edge))
    def _():
        pl.semaphore_wait(barrier, bands - 1)

    def near(other):
        return remote(
            replies.at[0],
            gathered.at[band + 1],
            send_sems.at[other],
            recv_sems.at[band + 1],
            first + other,
        )

    def far_after(other):
        return remote(
            replies.at[1],
            gathered.at[0],
            send_sems.at[bands + other],
            recv_sems.at[0],
            after + other,
        )

    def far_before(other):
        return remote(
            replies.at[1],
            gathered.at[bands + 1],
            send_sems.at[bands + other],
            recv_sems.at[bands + 1],
            before + other,
        )

    def arriving(part):
        return remote(
            replies.at[0], gathered.at[part], send_sems.at[0], recv_sems.at[part], first
        )

    for other in range(bands):
        @pl.when(band == 0)
        def _():
            far_before(other).start()

        @pl.when(band == bands - 1)
        def _():
            far_after(other).start()

        @pl.when(band != other)
        def _():
            near(other).start()
    gathered[pl.ds(band + 1, 1)] = replies[pl.ds(0, 1)]
    for part in (0, bands + 1):
        arriving(part).wait_recv()
    for other in range(bands):
        @pl.when(band != other)
        def _():
            arriving(other + 1).wait_recv()
            near(other).wait_send()

        @pl.when(band == 0)
        def _():
            far_before(other).wait_send()

        @pl.when(band == bands - 1)
        def _():
            far_after(other).wait_send()


def context_part(wide, probs, grad, start, count):
    channels = grad.shape[0]

    def add(depth, sums):
        weight = probs[pl.ds(depth, 1)][0]
        return tuple(
            held + wide[pl.ds(depth * channels + start + step, 1), :] * weight
            for step, held in enumerate(sums)
        )

    zero = jnp.zeros(probs.shape[1:], jnp.float32)
    sums = lax.fori_loop(0, probs.shape[0], add, (zero,) * count, unroll=2)
    for step, held in enumerate(sums):
        grad[start + step] = held.astype(grad.dtype)


def prob_part(wide, features, probs, grad, mean, start, count):
    channels = features.shape[0]

    def add(channel, sums):
        feature = features[pl.ds(channel, 1)][0]
        return tuple(
            held + wide[pl.ds((start + step) * channels + channel, 1), :] * feature
            for step, held in enumerate(sums)
        )

    zero = jnp.zeros(probs.shape[1:], jnp.float32)
    sums = lax.fori_loop(0, channels, add, (zero,) * count, unroll=2)
    total = mean[...]
    for step, held in enumerate(sums):
        grad[start + step] = held
        total = total + probs[start + step] * held
    mean[...] = total


def logit_part(probs, lidar, grad, mean):
    named = lidar[...]
    kept = (named >= 0).astype(jnp.float32)
    expected = mean[...]

    def one(depth, carry):
        prob = probs[pl.ds(depth, 1)][0]
        hit = (named == depth).astype(jnp.float32)
        value = prob * (grad[pl.ds(depth, 1)][0] - expected) + DEPTH_WEIGHT * (
            kept * prob - hit
        )
        grad[pl.ds(depth, 1)] = value[None]
        return carry

    lax.fori_loop(0, probs.shape[0], one, 0, unroll=2)


def sum_kernel(
    chips, terms, wide, probs, context, lidar, out, logit_grad, context_grad,
    features, mean, pair, local, stage_r, stage_l, land_r, land_l,
    pair_sems, ring_r, ring_l, pass_r, pass_l,
):
    me = lax.axis_index("blk")
    core = me % 2
    chip = me // 2
    blocks = 2 * chips
    partner = me + 1 - 2 * core
    right = (me + 2) % blocks
    left = (me + blocks - 2) % blocks
    rights = chips // 2
    lefts = chips - 1 - rights
    barrier = pltpu.get_barrier_semaphore()
    for other in (partner, right, left):
        greet(barrier, other)
    pl.semaphore_wait(barrier, 3)
    swap = remote(terms.at[1 - core], pair, pair_sems.at[0], pair_sems.at[1], partner)
    swap.start()
    features[...] = context[...].astype(jnp.float32)
    mean[...] = jnp.zeros_like(mean)
    parts = 2 * rights
    depths = probs.shape[0] // parts
    widths = context.shape[0] // parts
    swap.wait_recv()
    local[...] = (
        terms[pl.ds(core, 1)][0].astype(jnp.float32) + pair[...].astype(jnp.float32)
    )
    moves_r = []
    moves_l = []
    for step in range(rights):
        chunk = (chip + rights - step) % chips
        value = local[pl.ds(chunk, 1)][0]
        if step:
            moves_r[-1].wait_recv()
            value = value + land_r[step - 1].astype(jnp.float32)
        stage_r[step] = value.astype(stage_r.dtype)
        move = remote(
            stage_r.at[step], land_r.at[step], ring_r.at[0, step], ring_r.at[1, step], right
        )
        move.start()
        moves_r.append(move)
        if step < lefts:
            chunk = (chip + chips - lefts + step) % chips
            value = local[pl.ds(chunk, 1)][0]
            if step:
                moves_l[-1].wait_recv()
                value = value + land_l[step - 1].astype(jnp.float32)
            stage_l[step] = value.astype(stage_l.dtype)
            move = remote(
                stage_l.at[step], land_l.at[step], ring_l.at[0, step], ring_l.at[1, step], left
            )
            move.start()
            moves_l.append(move)
        for part in (2 * step, 2 * step + 1):
            context_part(wide, probs, context_grad, part * widths, widths)
    moves_l[-1].wait_recv()
    moves_r[-1].wait_recv()
    total = (
        local[pl.ds(chip, 1)][0]
        + land_r[rights - 1].astype(jnp.float32)
        + land_l[lefts - 1].astype(jnp.float32)
    )
    out[pl.ds(core, 1), pl.ds(chip, 1)] = total.astype(out.dtype)[None, None]

    def passing_r(step, origin):
        block = out.at[core, (origin + chips - step) % chips]
        return remote(block, block, pass_r.at[0, step], pass_r.at[1, step], right)

    def passing_l(step, origin):
        block = out.at[core, (origin + step) % chips]
        return remote(block, block, pass_l.at[0, step], pass_l.at[1, step], left)

    for step in range(rights):
        if step:
            passing_r(step - 1, chip + chips - 1).wait_recv()
        passing_r(step, chip).start()
        if step < lefts:
            if step:
                passing_l(step - 1, chip + 1).wait_recv()
            passing_l(step, chip).start()
        for part in (2 * step, 2 * step + 1):
            prob_part(wide, features, probs, logit_grad, mean, part * depths, depths)
    passing_l(lefts - 1, chip + 1).wait_recv()
    passing_r(rights - 1, chip + chips - 1).wait_recv()
    whole = remote(
        out.at[core], out.at[core], pair_sems.at[2], pair_sems.at[3], partner
    )
    whole.start()
    logit_part(probs, lidar, logit_grad, mean)
    remote(
        out.at[1 - core], out.at[1 - core], pair_sems.at[2], pair_sems.at[3], partner
    ).wait_recv()
    whole.wait_send()
    swap.wait_send()
    for move in moves_r + moves_l:
        move.wait_send()
    for step in range(rights):
        passing_r(step, chip).wait_send()
    for step in range(lefts):
        passing_l(step, chip).wait_send()


VMEM = pl.BlockSpec(memory_space=pltpu.VMEM)


def scatter_pieces(pieces, bands):
    blocks = lax.axis_size("blk")
    shape = pieces.shape[1:]

    def kernel(*refs):
        scatter_kernel(blocks, bands, *refs)

    return pl.pallas_call(
        kernel,
        out_shape=jax.ShapeDtypeStruct((2,) + shape, pieces.dtype),
        in_specs=[VMEM],
        out_specs=VMEM,
        scratch_shapes=[
            pltpu.VMEM((2 * bands,) + shape, pieces.dtype),
            pltpu.SemaphoreType.DMA((bands + 2,)),
            pltpu.SemaphoreType.DMA((2 * bands,)),
        ],
        compiler_params=pltpu.CompilerParams(collective_id=0, has_side_effects=True),
        name="scatter_pieces",
    )(pieces)


def gather_replies(replies, bands):
    blocks = lax.axis_size("blk")
    shape = replies.shape[1:]

    def kernel(*refs):
        reply_kernel(blocks, bands, *refs)

    return pl.pallas_call(
        kernel,
        out_shape=jax.ShapeDtypeStruct((bands + 2,) + shape, replies.dtype),
        in_specs=[VMEM],
        out_specs=VMEM,
        scratch_shapes=[
            pltpu.SemaphoreType.DMA((2 * bands,)),
            pltpu.SemaphoreType.DMA((bands + 2,)),
        ],
        compiler_params=pltpu.CompilerParams(collective_id=1, has_side_effects=True),
        name="gather_replies",
    )(replies)


def summed(terms, wide, probs, context, lidar):
    chips = terms.shape[1]
    rights = chips // 2
    lefts = chips - 1 - rights
    block = terms.shape[2:]
    kind = terms.dtype

    def kernel(*refs):
        sum_kernel(chips, *refs)

    return pl.pallas_call(
        kernel,
        out_shape=(
            jax.ShapeDtypeStruct(terms.shape, kind),
            jax.ShapeDtypeStruct(probs.shape, jnp.float32),
            jax.ShapeDtypeStruct(context.shape, context.dtype),
        ),
        in_specs=[VMEM] * 5,
        out_specs=(VMEM,) * 3,
        scratch_shapes=[
            pltpu.VMEM(context.shape, jnp.float32),
            pltpu.VMEM(probs.shape[1:], jnp.float32),
            pltpu.VMEM((chips,) + block, kind),
            pltpu.VMEM((chips,) + block, jnp.float32),
            pltpu.VMEM((rights,) + block, kind),
            pltpu.VMEM((lefts,) + block, kind),
            pltpu.VMEM((rights,) + block, kind),
            pltpu.VMEM((lefts,) + block, kind),
            pltpu.SemaphoreType.DMA((4,)),
            pltpu.SemaphoreType.DMA((2, rights)),
            pltpu.SemaphoreType.DMA((2, lefts)),
            pltpu.SemaphoreType.DMA((2, rights)),
            pltpu.SemaphoreType.DMA((2, lefts)),
        ],
        compiler_params=pltpu.CompilerParams(collective_id=2, has_side_effects=True),
        name="sum_gradients",
    )(terms, wide, probs, context, lidar)


def tripled(field):
    length = field.shape[1]
    padded = jnp.pad(field, ((0, 0), (1, 1), (0, 0)))
    return jnp.concatenate([padded[:, col : col + length] for col in range(3)], axis=2)


def conv_rows(triple, weight):
    height = triple.shape[0] - 2
    length = triple.shape[1]
    wide = jnp.concatenate([triple[row : row + height] for row in range(3)], axis=2)
    flat = wide.reshape(height * length, -1)
    return jnp.dot(
        flat, weight.reshape(-1, weight.shape[3]), preferred_element_type=jnp.float32
    ).reshape(height, length, weight.shape[3])


def weight_grad(triple, upstream):
    height, length, width = upstream.shape
    flat = upstream.reshape(height * length, width)
    rows = []
    for row in range(3):
        left = triple[row : row + height].reshape(height * length, -1)
        rows.append(
            lax.dot_general(
                left, flat, (((0,), (0,)), ((), ())), preferred_element_type=jnp.float32
            ).astype(jnp.bfloat16)
        )
    return jnp.concatenate(rows, axis=0)


def mirrored(weight):
    return jnp.flip(weight, (0, 1)).transpose(0, 1, 3, 2)


def shards(
    depth_logits, context, lidar_bins, az_map, rng_map, conv1_weight, conv2_weight, out_grad
):
    blocks = lax.axis_size("blk")
    position = lax.axis_index("blk")
    cameras = az_map.shape[0]
    bands = blocks // cameras
    sector, length, hidden_width = out_grad.shape
    bin_count = depth_logits.shape[1]
    channels = context.shape[1]
    columns = depth_logits.shape[3]
    camera = position // bands
    band = position % bands
    upstream_wide = with_halo(out_grad, 2)
    depth_prob = jax.nn.softmax(depth_logits[0], axis=0)
    probs_low = depth_prob.astype(jnp.bfloat16)
    view_context = context[0]
    wedge = jnp.einsum("brc,hrc->cbh", probs_low, view_context, preferred_element_type=jnp.float32)
    wedge = wedge.astype(jnp.bfloat16).reshape(columns, bin_count * channels)
    az_row = lax.dynamic_slice_in_dim(az_map, camera, 1, 0)[0]
    span = (bands + 2) * sector
    seen = ((camera * bands + blocks - 1) * sector + jnp.arange(span, dtype=jnp.int32)) % (
        blocks * sector
    )
    column_hot = (seen[:, None] == az_row[None, :]).astype(jnp.bfloat16)
    pieces = jnp.dot(column_hot, wedge, preferred_element_type=jnp.float32).astype(jnp.bfloat16)
    sums = scatter_pieces(pieces.reshape(bands + 2, sector, bin_count * channels), bands)
    neighbour = jnp.where(band == 0, camera + cameras - 1, camera + 1) % cameras
    cells = jnp.arange(length, dtype=jnp.int32)
    ranges = jnp.concatenate(
        [
            lax.dynamic_slice_in_dim(rng_map, camera, 1, 0),
            lax.dynamic_slice_in_dim(rng_map, neighbour, 1, 0),
        ],
        axis=0,
    )
    range_hot = (ranges[:, None, :] == cells[None, :, None]).astype(jnp.bfloat16)
    bev = jnp.einsum(
        "nrb,nabh->arh",
        range_hot,
        sums.reshape(2, sector, bin_count, channels),
        preferred_element_type=jnp.float32,
    ).astype(jnp.bfloat16)
    bev_triple = tripled(with_halo(bev, 2))
    hidden_pre = conv_rows(bev_triple, conv1_weight)
    activated = jax.nn.silu(hidden_pre).astype(jnp.bfloat16)
    conv2_grad = weight_grad(tripled(activated), out_grad)
    act_grad = conv_rows(tripled(upstream_wide), mirrored(conv2_weight))
    pre_grad = (act_grad * silu_slope(hidden_pre)).astype(jnp.bfloat16)
    conv1_grad = weight_grad(bev_triple[1:-1], pre_grad[1:-1])
    bev_grad = conv_rows(tripled(pre_grad), mirrored(conv1_weight)).astype(jnp.bfloat16)
    replies = jnp.einsum(
        "nrb,arh->nabh", range_hot, bev_grad, preferred_element_type=jnp.float32
    ).astype(jnp.bfloat16)
    gathered = gather_replies(replies.reshape(2, sector, bin_count * channels), bands)
    wide = lax.dot_general(
        gathered.reshape(span, bin_count * channels),
        column_hot,
        (((0,), (0,)), ((), ())),
        preferred_element_type=jnp.float32,
    )
    rows1 = conv1_grad.shape[0]
    rows2 = conv2_grad.shape[0]
    step = 16 * blocks
    padding = -(rows1 + rows2) % step
    terms = jnp.concatenate(
        [conv1_grad, conv2_grad, jnp.zeros((padding, hidden_width), jnp.bfloat16)], axis=0
    )
    terms, logit_grad, context_grad = summed(
        terms.reshape(2, blocks // 2, -1, hidden_width),
        wide,
        depth_prob,
        view_context,
        lidar_bins[0],
    )
    terms = terms.reshape(-1, hidden_width).astype(jnp.float32)
    return (
        logit_grad[None],
        context_grad[None],
        terms[:rows1].reshape(3, 3, channels, hidden_width),
        terms[rows1 : rows1 + rows2].reshape(3, 3, hidden_width, hidden_width),
    )


def solution(mesh):
    return jax.shard_map(
        shards,
        mesh=mesh,
        in_specs=(
            P(("group", "blk"), None, None, None),
            P(("group", "blk"), None, None, None),
            P(("group", "blk"), None, None),
            P(),
            P(),
            P(),
            P(),
            P(("group", "blk"), None, None),
        ),
        out_specs=(
            P(("group", "blk"), None, None, None),
            P(("group", "blk"), None, None, None),
            P("group", None, None, None),
            P("group", None, None, None),
        ),
        check_vma=False,
    )
```

profile of v0, /device:TPU:69, one launch (start us, length us, event | category | flops | bytes accessed | tf_op | source)
XLA Modules:
  0.0 223.5 jit_solution(15900769249249529758)
XLA Ops:
  0.6 0.0 copy-start
  0.6 0.0 copy-start.2
  0.7 1.8 reduce_max.9
  2.5 1.8 fusion.24
  4.3 1.6 fusion.97
  5.9 2.1 copy.19
  8.1 1.9 copy.20
  10.0 2.4 %convolution_convert_fusion.1 = bf16[128,112,80]{1,2,0:T(8,128)(2,1)S(1)} fusion(bf16[112,32,128]{0,1,2:T(8,128)(2,1)} %copy.19, bf16[80,32,128]{0,1,2:T(8,128)(2,1)} %copy.20), kind=kOutput, calls=%fused_computation.36 | convolution fusion | flops 74547200 | bytes 3866624 | tf_op jit(solution)/shard_map/brc,hrc->cbh/dot_general | solution.py:497
  12.4 3.8 %copy.21 = bf16[128,112,80]{0,2,1:T(8,128)(2,1)} copy(bf16[128,112,80]{1,2,0:T(8,128)(2,1)S(1)} %convolution_convert_fusion.1) | data formatting | bytes 4587520 | tf_op jit(solution)/shard_map/convert_element_type | solution.py:498
  16.2 0.0 copy-start.3
  16.2 3.7 %fusion.12.refs_0_ = bf16[6,8,8960]{2,1,0:T(8,128)(2,1)} fusion(bf16[128,8960]{0,1:T(8,128)(2,1)} %bitcast.109, s32[128]{0:T(128)S(1)} %fusion.92, s32[48]{0:T(128)S(1)} %and_select_fusion), kind=kOutput, calls=%fused_computation.13 | convolution fusion | flops 110536704 | bytes 3154624 | tf_op jit(solution)/shard_map/dot_general | solution.py:505
  19.9 26.5 %scatter_pieces.1 = bf16[2,8,8960]{2,1,0:T(8,128)(2,1)} custom-call(bf16[6,8,8960]{2,1,0:T(8,128)(2,1)} %fusion.12.refs_0_), custom_call_target="tpu_custom_call" | custom-call | tf_op jit(solution)/shard_map/scatter_pieces/pallas_call | solution.py:371
  46.4 1.7 reshape.84
  48.2 0.8 constant_dynamic-slice_fusion.1
  49.0 0.4 fusion.38
  49.4 0.1 collective-permute-start
  49.5 0.5 collective-permute-start.1
  50.0 1.0 fusion.102
  51.0 1.3 collective-permute-start.2
  52.3 1.6 copy.23
  53.9 1.1 rev.8
  55.0 1.0 reverse_bitcast_fusion
  56.0 0.3 copy.27
  56.3 1.2 reshape.104
  57.5 0.7 fusion.49
  58.1 0.5 fusion.103
  58.7 0.2 pad_maximum_fusion.3
  58.9 0.8 fusion.101
  59.8 0.1 copy-done.8
  59.9 0.3 copy-done.20
  60.2 4.6 %multiply_convert_fusion = (bf16[10,512,256]{2,1,0:T(8,128)(2,1)S(1)}, f32[10,512,256]{2,1,0:T(8,128)}) fusion(bf16[720,256,1]{1,0,2:T(8,128)(2,1)S(1)} %bitcast.117, bf16[10,512,240]{1,2,0:T(8,128)(2,1)S(1)} %get-tuple-element.22, bf16[10,512,240]{1,2,0:T(8,128)(2,1)S(1)} %get-tuple-element.21, bf16[10,512,240]{1,2,0:T(8,128)(2,1)S(1)} %get-tuple-element.20), kind=kOutput, calls=%fused_computation.23 | convolution fusion | flops 1916108800 | bytes 15605760 | tf_op jit(solution)/shard_map/dot_general | solution.py:457
  64.8 3.5 %pad_slice_fusion.5 = (bf16[10,512,256]{2,1,0:T(8,128)(2,1)}, bf16[10,512,256]{2,1,0:T(8,128)(2,1)}) fusion(bf16[10,512,256]{2,1,0:T(8,128)(2,1)S(1)} %get-tuple-element.35), kind=kLoop, calls=%fused_computation.35 | loop fusion | bytes 7864320 | tf_op jit(solution)/shard_map/slice | solution.py:449
  68.3 1.1 constant_dynamic-update-slice_fusion.2
  69.4 0.1 constant_dynamic-update-slice_fusion.1
  69.6 1.5 pad_slice_fusion.1
  71.1 1.0 pad_maximum_fusion
  72.1 8.4 %fusion.99 = (bf16[10,512,768]{2,1,0:T(8,128)(2,1)}, bf16[10,512,768]{2,1,0:T(8,128)(2,1)}, bf16[10,512,768]{2,1,0:T(8,128)(2,1)}) fusion(bf16[12,512,768]{2,1,0:T(8,128)(2,1)S(1)} %pad_maximum_fusion), kind=kLoop, calls=%fused_computation.109 | loop fusion | bytes 47185920 | tf_op jit(solution)/shard_map/slice | solution.py:455
  80.5 12.8 %multiply_convert_fusion.1 = bf16[10,512,256]{2,1,0:T(8,128)(2,1)S(1)} fusion(f32[10,512,256]{2,1,0:T(8,128)} %get-tuple-element.36, bf16[2304,256,1]{1,0,2:T(8,128)(2,1)S(1)} %bitcast.114, bf16[10,512,768]{2,1,0:T(8,128)(2,1)} %get-tuple-element.13, bf16[10,512,768]{2,1,0:T(8,128)(2,1)} %get-tuple-element.14, bf16[10,512,768]{2,1,0:T(8,128)(2,1)} %get-tuple-element.12), kind=kOutput, calls=%fused_computation.24 | convolution fusion | flops 6122373120 | bytes 32636928 | tf_op jit(solution)/shard_map/dot_general | solution.py:457
  93.3 1.1 pad_slice_fusion.3
  94.5 0.6 pad_maximum_fusion.2
  95.1 6.8 %fusion.100 = (bf16[8,512,768]{2,1,0:T(8,128)(2,1)}, bf16[8,512,768]{2,1,0:T(8,128)(2,1)}, bf16[8,512,768]{2,1,0:T(8,128)(2,1)}) fusion(bf16[10,512,768]{2,1,0:T(8,128)(2,1)S(1)} %pad_maximum_fusion.2), kind=kLoop, calls=%fused_computation.110 | loop fusion | bytes 37748736 | tf_op jit(solution)/shard_map/slice | solution.py:455
  101.9 9.7 %fusion.39 = bf16[8,512,80,1]{1,2,3,0:T(8,128)(2,1)S(1)} fusion(bf16[2304,80,1]{0,1,2:T(8,128)(2,1)S(1)} %copy-done.21, bf16[8,512,768]{2,1,0:T(8,128)(2,1)} %get-tuple-element.16, bf16[8,512,768]{2,1,0:T(8,128)(2,1)} %get-tuple-element.17, bf16[8,512,768]{2,1,0:T(8,128)(2,1)} %get-tuple-element.15), kind=kOutput, calls=%fused_computation.58 | convolution fusion | flops 1566900224 | bytes 19898368 | tf_op jit(solution)/shard_map/dot_general | solution.py:457
  111.6 1.2 fusion.50
  112.8 1.9 copy.28
  114.7 2.2 reshape.89.refs_0_
  116.9 16.3 %gather_replies.1 = bf16[6,8,8960]{2,1,0:T(8,128)(2,1)} custom-call(bf16[2,8,8960]{2,1,0:T(8,128)(2,1)} %reshape.89.refs_0_), custom_call_target="tpu_custom_call" | custom-call | tf_op jit(solution)/shard_map/gather_replies/pallas_call | solution.py:393
  133.2 4.2 %fusion.78.refs_1_ = f32[8960,128]{1,0:T(8,128)} fusion(bf16[6,8,8960]{2,1,0:T(8,128)(2,1)} %gather_replies.1, s32[128]{0:T(128)S(1)} %fusion.92, s32[48]{0:T(128)S(1)} %and_select_fusion), kind=kOutput, calls=%fused_computation.78 | convolution fusion | flops 110106624 | bytes 5448384 | tf_op jit(solution)/shard_map/dot_general | solution.py:535
  137.5 1.3 fusion.75
  138.8 1.3 fusion.69
  140.2 1.3 fusion.63
  141.5 0.2 copy-done.5
  141.7 0.8 copy-done.12
  142.6 0.8 copy-done.13
  143.4 0.7 copy-done.14
  144.1 2.6 %fusion.43 = bf16[3072,256]{1,0:T(8,128)(2,1)} fusion(bf16[3072,256]{1,0:T(8,128)(2,1)} %fusion.63, bf16[8,512,256]{2,1,0:T(8,128)(2,1)S(1)} %copy-done.5, bf16[10,512,256]{2,1,0:T(8,128)(2,1)S(1)} %copy-done.14, bf16[10,512,256]{2,1,0:T(8,128)(2,1)S(1)} %copy-done.12, bf16[10,512,256]{2,1,0:T(8,128)(2,1)S(1)} %copy-done.13), kind=kOutput, calls=%fused_computation.60 | convolution fusion | flops 1634402304 | bytes 10354688 | tf_op jit(solution)/shard_map/dot_general | solution.py:469
  146.7 2.6 %fusion.45 = bf16[3072,256]{1,0:T(8,128)(2,1)} fusion(bf16[3072,256]{1,0:T(8,128)(2,1)} %fusion.43, bf16[8,512,256]{2,1,0:T(8,128)(2,1)S(1)} %copy-done.5, bf16[10,512,256]{2,1,0:T(8,128)(2,1)S(1)} %copy-done.14, bf16[10,512,256]{2,1,0:T(8,128)(2,1)S(1)} %copy-done.12, bf16[10,512,256]{2,1,0:T(8,128)(2,1)S(1)} %copy-done.13), kind=kOutput, calls=%fused_computation.62 | convolution fusion | flops 1634402304 | bytes 10354688 | tf_op jit(solution)/shard_map/dot_general | solution.py:469
  149.3 2.6 %fusion.47 = bf16[3072,256]{1,0:T(8,128)(2,1)} fusion(bf16[3072,256]{1,0:T(8,128)(2,1)} %fusion.45, bf16[8,512,256]{2,1,0:T(8,128)(2,1)S(1)} %copy-done.5, bf16[10,512,256]{2,1,0:T(8,128)(2,1)S(1)} %copy-done.14, bf16[10,512,256]{2,1,0:T(8,128)(2,1)S(1)} %copy-done.12, bf16[10,512,256]{2,1,0:T(8,128)(2,1)S(1)} %copy-done.13), kind=kOutput, calls=%fused_computation.64 | convolution fusion | flops 1634402304 | bytes 10354688 | tf_op jit(solution)/shard_map/dot_general | solution.py:469
  151.9 0.6 constant_dynamic-update-slice_fusion.3
  152.5 64.8 %sum_gradients.1 = (bf16[2,16,96,256]{3,2,1,0:T(8,128)(2,1)}, f32[112,32,128]{2,1,0:T(8,128)}, bf16[80,32,128]{2,1,0:T(8,128)(2,1)}) custom-call(bf16[2,16,96,256]{3,2,1,0:T(8,128)(2,1)} %bitcast.20.refs_0_, f32[8960,128]{1,0:T(8,128)} %fusion.78.refs_1_, f32[112,32,128]{2,1,0:T(8,128)} %get-tuple-element.11.refs_2_, bf16[80,32,128]{2,1,0:T(8,128)(2,1)} %bitcast.110, ...), custom_call_target="tpu_custom_call" | custom-call | tf_op jit(solution)/shard_map/sum_gradients/pallas_call | solution.py:417
  217.3 1.6 bitcast_convert_fusion
  219.0 1.6 slice.143
  220.6 0.9 slice.142
  221.5 1.2 copy.45
  222.7 0.8 copy.46
  (45 shorter events, 0.2 us)
Async XLA Ops:
  0.6 15.6 %copy-start = (s32[8,128]{1,0:T(8,128)S(1)}, s32[8,128]{1,0:T(8,128)}, u32[]{:S(2)}) copy-start(s32[8,128]{1,0:T(8,128)} %param.11) | copy-start | bytes 12292
  0.6 3.7 %copy-start.2 = (f32[1,112,32,128]{3,2,1,0:T(8,128)S(1)}, f32[1,112,32,128]{3,2,1,0:T(8,128)}, u32[]{:S(2)}) copy-start(f32[1,112,32,128]{3,2,1,0:T(8,128)} %param.8) | copy-start | bytes 5505028
  4.3 3.8 %copy-start.10 = (bf16[1,80,32,128]{3,2,1,0:T(8,128)(2,1)S(1)}, bf16[1,80,32,128]{3,2,1,0:T(8,128)(2,1)}, u32[]{:S(2)}) copy-start(bf16[1,80,32,128]{3,2,1,0:T(8,128)(2,1)} %param.9) | copy-start | bytes 1966084
  16.2 33.8 %copy-start.3 = (bf16[8,512,256]{2,1,0:T(8,128)(2,1)S(1)}, bf16[8,512,256]{2,1,0:T(8,128)(2,1)}, u32[]{:S(2)}) copy-start(bf16[8,512,256]{2,1,0:T(8,128)(2,1)} %param.15) | copy-start | bytes 6291460
  49.4 8.0 %collective-permute-start = (bf16[2,512,80]{1,2,0:T(8,128)(2,1)S(1)}, bf16[2,512,80]{1,2,0:T(8,128)(2,1)S(1)}, u32[]{:S(2)}, u32[]{:S(2)}) collective-permute-start(bf16[2,512,80]{1,2,0:T(8,128)(2,1)S(1)} %get-tuple-element.31), channel_id=1, source_target_pairs={{0,1},{1,2},{2,3},{3,4},{4,5},{5,6},{6,7},{7,8},{8,9},{9,10},{10,1... | collective-permute-start | bytes 491528 | tf_op jit(solution)/shard_map/ppermute | solution.py:17
  49.5 7.9 %collective-permute-start.1 = (bf16[2,512,80]{1,2,0:T(8,128)(2,1)S(1)}, bf16[2,512,80]{1,2,0:T(8,128)(2,1)S(1)}, u32[]{:S(2)}, u32[]{:S(2)}) collective-permute-start(bf16[2,512,80]{1,2,0:T(8,128)(2,1)S(1)} %get-tuple-element.32), channel_id=1, source_target_pairs={{1,0},{2,1},{3,2},{4,3},{5,4},{6,5},{7,6},{8,7},{9,8},{10,9},{11,1... | collective-permute-start | bytes 491528 | tf_op jit(solution)/shard_map/ppermute | solution.py:19
  51.0 17.3 %collective-permute-start.2 = (bf16[2,512,256]{2,1,0:T(8,128)(2,1)}, bf16[2,512,256]{2,1,0:T(8,128)(2,1)}, u32[]{:S(2)}, u32[]{:S(2)}) collective-permute-start(bf16[2,512,256]{2,1,0:T(8,128)(2,1)} %get-tuple-element.28), channel_id=1, source_target_pairs={{0,1},{1,2},{2,3},{3,4},{4,5},{5,6},{6,7},{7,8},{8,9},{9,10},{10,1... | collective-permute-start | bytes 1572872 | tf_op jit(solution)/shard_map/ppermute | solution.py:17
  52.3 17.2 %collective-permute-start.3 = (bf16[2,512,256]{2,1,0:T(8,128)(2,1)}, bf16[2,512,256]{2,1,0:T(8,128)(2,1)S(1)}, u32[]{:S(2)}, u32[]{:S(2)}) collective-permute-start(bf16[2,512,256]{2,1,0:T(8,128)(2,1)} %get-tuple-element.27), channel_id=1, source_target_pairs={{1,0},{2,1},{3,2},{4,3},{5,4},{6,5},{7,6},{8,7},{9,8},{10,9},{11,1... | collective-permute-start | bytes 1572872 | tf_op jit(solution)/shard_map/ppermute | solution.py:19
  57.5 1.5 copy-start.17
  58.6 1.1 copy-start.6
  58.7 1.3 copy-start.8
  58.9 1.3 copy-start.20
  64.8 3.5 %copy-start.11 = (bf16[10,512,256]{2,1,0:T(8,128)(2,1)}, bf16[10,512,256]{2,1,0:T(8,128)(2,1)S(1)}, u32[]{:S(2)}) copy-start(bf16[10,512,256]{2,1,0:T(8,128)(2,1)S(1)} %get-tuple-element.35) | copy-start | bytes 7864324
  64.8 4.6 %copy-start.4 = (bf16[8,512,256]{2,1,0:T(8,128)(2,1)S(1)}, bf16[8,512,256]{2,1,0:T(8,128)(2,1)}, u32[]{:S(2)}) copy-start(bf16[8,512,256]{2,1,0:T(8,128)(2,1)} %param.15) | copy-start | bytes 6291460
  72.1 8.4 %copy-start.16 = (bf16[3,3,256,256]{2,3,1,0:T(8,128)(2,1)S(1)}, bf16[3,3,256,256]{2,3,1,0:T(8,128)(2,1)}, u32[]{:S(2)}) copy-start(bf16[3,3,256,256]{2,3,1,0:T(8,128)(2,1)} %rev.8) | copy-start | bytes 3538948
  95.1 6.9 %copy-start.21 = (bf16[2304,80,1]{0,1,2:T(8,128)(2,1)S(1)}, bf16[2304,80,1]{0,1,2:T(8,128)(2,1)}, u32[]{:S(2)}) copy-start(bf16[2304,80,1]{0,1,2:T(8,128)(2,1)} %reshape.104) | copy-start | bytes 1105924
  133.2 4.3 %copy-start.7 = (bf16[12,512,80]{1,2,0:T(8,128)(2,1)S(1)}, bf16[12,512,80]{1,2,0:T(8,128)(2,1)}, u32[]{:S(2)}) copy-start(bf16[12,512,80]{1,2,0:T(8,128)(2,1)} %copy-done.6) | copy-start | bytes 2949124
  133.2 4.3 %copy-start.9 = (bf16[12,512,80]{1,2,0:T(8,128)(2,1)S(1)}, bf16[12,512,80]{1,2,0:T(8,128)(2,1)}, u32[]{:S(2)}) copy-start(bf16[12,512,80]{1,2,0:T(8,128)(2,1)} %copy-done.8) | copy-start | bytes 2949124
  133.2 4.3 %copy-start.18 = (bf16[2,512,80]{1,2,0:T(8,128)(2,1)S(1)}, bf16[2,512,80]{1,2,0:T(8,128)(2,1)}, u32[]{:S(2)}) copy-start(bf16[2,512,80]{1,2,0:T(8,128)(2,1)} %copy-done.17) | copy-start | bytes 491524
  140.2 1.6 copy-start.5
  140.2 2.4 %copy-start.12 = (bf16[10,512,256]{2,1,0:T(8,128)(2,1)S(1)}, bf16[10,512,256]{2,1,0:T(8,128)(2,1)}, u32[]{:S(2)}) copy-start(bf16[10,512,256]{2,1,0:T(8,128)(2,1)} %copy-done.11) | copy-start | bytes 7864324
  140.2 3.2 %copy-start.13 = (bf16[10,512,256]{2,1,0:T(8,128)(2,1)S(1)}, bf16[10,512,256]{2,1,0:T(8,128)(2,1)}, u32[]{:S(2)}) copy-start(bf16[10,512,256]{2,1,0:T(8,128)(2,1)} %get-tuple-element.25) | copy-start | bytes 7864324
  140.2 4.0 %copy-start.14 = (bf16[10,512,256]{2,1,0:T(8,128)(2,1)S(1)}, bf16[10,512,256]{2,1,0:T(8,128)(2,1)}, u32[]{:S(2)}) copy-start(bf16[10,512,256]{2,1,0:T(8,128)(2,1)} %get-tuple-element.26) | copy-start | bytes 7864324
  219.0 2.5 %copy-start.15 = (f32[112,32,128]{2,1,0:T(8,128)S(1)}, f32[112,32,128]{2,1,0:T(8,128)}, u32[]{:S(2)}) copy-start(f32[112,32,128]{2,1,0:T(8,128)} %get-tuple-element.7) | copy-start | bytes 5505028
  219.0 4.6 %copy-start.1 = (s32[8,128]{1,0:T(8,128)S(1)}, s32[8,128]{1,0:T(8,128)}, u32[]{:S(2)}) copy-start(s32[8,128]{1,0:T(8,128)} %param.11) | copy-start | bytes 12292
  220.6 2.1 copy-start.19
where the time goes:
time: 224 us
  Pallas kernels  108 us (48%)
  local copies, waits for them, and re-layouts  52.8 us (24%)
  matrix products  50.7 us (23%)
  other arithmetic  9.39 us (4%)
    pallas_call x1, Pallas kernels, summed(): pl.pallas_call(kernel, out_shape=(jax.ShapeDtypeStruct(terms.shape, kind)...  64.8 us
    dot_general x3, matrix products, conv_rows(): jnp.dot(flat, weight.reshape(-1, weight.shape[3]), preferred_element_type...  27 us
    pallas_call x1, Pallas kernels, scatter_pieces(): pl.pallas_call(kernel, out_shape=jax.ShapeDtypeStruct((2,) + shape, piece...  26.5 us
    pallas_call x1, Pallas kernels, gather_replies(): pl.pallas_call(kernel, out_shape=jax.ShapeDtypeStruct((bands + 2,) + shap...  16.3 us
    slice x3, local copies, waits for them, and re-layouts, conv_rows(): triple[row:row + height]  16.1 us
    dot_general x6, matrix products, weight_grad(): lax.dot_general(left, flat, (((0,), (0,)), ((), ())), preferred_element_t...  11.7 us
    unnamed x49, local copies, waits for them, and re-layouts  7.97 us
    slice x4, local copies, waits for them, and re-layouts, tripled(): padded[:, col:col + length]  6.66 us
  transfers between devices with their start and end apart: 4, of which 0 were waited for; matrix products, arithmetic and copies ran while one was open for 8% of the time, Pallas kernels for 0%

commit v1 on v0

--- a/solution.py
+++ b/solution.py
@@ -358,6 +358,81 @@
         passing_l(step, chip).wait_send()
 
 
+def slid(field, step):
+    length = field.shape[0]
+    moved = pltpu.roll(field, step % length, 0)
+    row = lax.broadcasted_iota(jnp.int32, field.shape, 0)
+    empty = 0 if step > 0 else length - 1
+    return jnp.where(row == empty, 0.0, moved)
+
+
+def back_taps(rows, weights):
+    columns = []
+    for tap_col in range(3):
+        total = None
+        for tap_row, row in enumerate(rows):
+            term = lax.dot_general(
+                row,
+                weights(tap_row, tap_col),
+                (((1,), (1,)), ((), ())),
+                preferred_element_type=jnp.float32,
+            )
+            total = term if total is None else total + term
+        columns.append(total)
+    return columns[1] + slid(columns[0], -1) + slid(columns[2], 1)
+
+
+def back_kernel(low, mid, high, hidden, weight2, weight1, pre, bev_grad, recent):
+    step = pl.program_id(0)
+    act_grad = back_taps(
+        (high[0], mid[0], low[0]), lambda row, col: weight2[row, col]
+    )
+    value = (act_grad * silu_slope(hidden[0])).astype(pre.dtype)
+    pre[0] = value
+    recent[pl.ds(step % 3, 1)] = value[None]
+
+    @pl.when(step >= 2)
+    def _():
+        rows = [recent[pl.ds((step + 3 - tap) % 3, 1)][0] for tap in range(3)]
+        grad = back_taps(rows, lambda row, col: weight1[row, col])
+        bev_grad[0] = grad[:, : bev_grad.shape[2]].astype(bev_grad.dtype)
+
+
+def backward(upstream_wide, hidden_pre, conv2_weight, conv1_weight):
+    height, length, width = hidden_pre.shape
+    channels = conv1_weight.shape[2]
+    weight1 = jnp.pad(conv1_weight, ((0, 0), (0, 0), (0, -channels % 128), (0, 0)))
+
+    def line(offset):
+        return pl.BlockSpec((1, length, width), lambda step: (step + offset, 0, 0))
+
+    def whole(array):
+        return pl.BlockSpec(array.shape, lambda step: (0,) * array.ndim)
+
+    return pl.pallas_call(
+        back_kernel,
+        grid=(height,),
+        out_shape=(
+            jax.ShapeDtypeStruct((height, length, width), jnp.bfloat16),
+            jax.ShapeDtypeStruct((height - 2, length, channels), jnp.bfloat16),
+        ),
+        in_specs=[
+            line(0), line(1), line(2), line(0), whole(conv2_weight), whole(weight1)
+        ],
+        out_specs=(
+            line(0),
+            pl.BlockSpec((1, length, channels), lambda step: (jnp.maximum(step - 2, 0), 0, 0)),
+        ),
+        scratch_shapes=[pltpu.VMEM((3, length, width), jnp.bfloat16)],
+        cost_estimate=pl.CostEstimate(
+            flops=2 * 9 * height * length * width * (width + 128),
+            bytes_accessed=16 * height * length * width,
+            transcendentals=height * length * width,
+        ),
+        name="backward_convs",
+    )(upstream_wide, upstream_wide, upstream_wide, hidden_pre, conv2_weight, weight1)
+
+
 VMEM = pl.BlockSpec(memory_space=pltpu.VMEM)
 
 
@@ -473,10 +548,6 @@
     return jnp.concatenate(rows, axis=0)
 
 
-def mirrored(weight):
-    return jnp.flip(weight, (0, 1)).transpose(0, 1, 3, 2)
-
-
 def shards(
     depth_logits, context, lidar_bins, az_map, rng_map, conv1_weight, conv2_weight, out_grad
 ):
@@ -524,10 +595,8 @@
     hidden_pre = conv_rows(bev_triple, conv1_weight)
     activated = jax.nn.silu(hidden_pre).astype(jnp.bfloat16)
     conv2_grad = weight_grad(tripled(activated), out_grad)
-    act_grad = conv_rows(tripled(upstream_wide), mirrored(conv2_weight))
-    pre_grad = (act_grad * silu_slope(hidden_pre)).astype(jnp.bfloat16)
+    pre_grad, bev_grad = backward(upstream_wide, hidden_pre, conv2_weight, conv1_weight)
     conv1_grad = weight_grad(bev_triple[1:-1], pre_grad[1:-1])
-    bev_grad = conv_rows(tripled(pre_grad), mirrored(conv1_weight)).astype(jnp.bfloat16)
     replies = jnp.einsum(
         "nrb,arh->nabh", range_hot, bev_grad, preferred_element_type=jnp.float32
     ).astype(jnp.bfloat16)

time: 224 us -> 195 us (0.87)
  local copies, waits for them, and re-layouts: 52.8 us -> 28.2 us
  matrix products: 50.7 us -> 29.5 us
  Pallas kernels: 108 us -> 125 us
    dot_general x3 -> x1, matrix products: 27 us -> 4.61 us  [conv_rows(): jnp.dot(flat, weight.reshape(-1, weight.shape[3]), preferred_element_type...]
    pallas_call x0 -> x1, Pallas kernels: none -> 18.3 us  [backward(): pl.pallas_call(back_kernel, grid=(height,), out_shape=(jax.ShapeDtypeStru...]
    slice x3 -> x1, local copies, waits for them, and re-layouts: 16.1 us -> 0.82 us  [conv_rows(): triple[row:row + height]]
    slice x4 -> x2, local copies, waits for them, and re-layouts: 6.66 us -> 4.11 us  [tripled(): padded[:, col:col + length]]
    unnamed x49 -> x36, local copies, waits for them, and re-layouts: 7.97 us -> 5.5 us
  transfers between devices with their start and end apart: 4 -> 4, of which waited for: 0 -> 1; matrix products, arithmetic and copies ran while one was open for 8% -> 6% of each run, Pallas kernels for 0% -> 0%
where the time goes in v1:
time: 195 us
  Pallas kernels  125 us (64%)
  matrix products  29.5 us (15%)
  local copies, waits for them, and re-layouts  28.2 us (14%)
  other arithmetic  8.17 us (4%)
    pallas_call x1, Pallas kernels, summed(): pl.pallas_call(kernel, out_shape=(jax.ShapeDtypeStruct(terms.shape, kind)...  64.9 us
    pallas_call x1, Pallas kernels, scatter_pieces(): pl.pallas_call(kernel, out_shape=jax.ShapeDtypeStruct((2,) + shape, piece...  26.9 us
    pallas_call x1, Pallas kernels, backward(): pl.pallas_call(back_kernel, grid=(height,), out_shape=(jax.ShapeDtypeStru...  18.3 us
    pallas_call x1, Pallas kernels, gather_replies(): pl.pallas_call(kernel, out_shape=jax.ShapeDtypeStruct((bands + 2,) + shap...  15.1 us
    dot_general x6, matrix products, weight_grad(): lax.dot_general(left, flat, (((0,), (0,)), ((), ())), preferred_element_t...  11.8 us
    unnamed x36, local copies, waits for them, and re-layouts  5.5 us
    dot_general x1, matrix products, conv_rows(): jnp.dot(flat, weight.reshape(-1, weight.shape[3]), preferred_element_type...  4.61 us
    dot_general x1, matrix products, shards(): lax.dot_general(gathered.reshape(span, bin_count * channels), column_hot,...  4.24 us
  transfers between devices with their start and end apart: 4, of which 1 were waited for; matrix products, arithmetic and copies ran while one was open for 6% of the time, Pallas kernels for 0%

profile of v1, /device:TPU:69, one launch (start us, length us, event | category | flops | bytes accessed | tf_op | source)
XLA Modules:
  0.0 194.8 jit_solution(1840032341107360361)
XLA Ops:
  0.6 0.0 copy-start
  0.6 0.0 copy-start.2
  0.7 1.8 reduce_max.9
  2.5 0.2 copy-done.2
  2.7 0.3 fusion.10
  3.0 1.6 fusion.76
  4.6 2.1 %copy.20 = bf16[112,32,128]{0,1,2:T(8,128)(2,1)} copy(bf16[112,32,128]{2,1,0:T(8,128)(2,1)S(1)} %get-tuple-element.14) | data formatting | bytes 1835008 | tf_op jit(solution)/shard_map/convert_element_type | solution.py:566
  6.8 0.0 copy-done.8
  6.8 1.9 copy.21
  8.7 2.4 %convolution_convert_fusion.1 = bf16[128,112,80]{1,2,0:T(8,128)(2,1)S(1)} fusion(bf16[112,32,128]{0,1,2:T(8,128)(2,1)} %copy.20, bf16[80,32,128]{0,1,2:T(8,128)(2,1)} %copy.21), kind=kOutput, calls=%fused_computation.17 | convolution fusion | flops 74547200 | bytes 3866624 | tf_op jit(solution)/shard_map/brc,hrc->cbh/dot_general | solution.py:568
  11.1 3.8 %copy.22 = bf16[128,112,80]{0,2,1:T(8,128)(2,1)} copy(bf16[128,112,80]{1,2,0:T(8,128)(2,1)S(1)} %convolution_convert_fusion.1) | data formatting | bytes 4587520 | tf_op jit(solution)/shard_map/convert_element_type | solution.py:569
  14.9 0.0 copy-done
  14.9 3.5 %fusion.refs_0_ = bf16[6,8,8960]{2,1,0:T(8,128)(2,1)} fusion(bf16[128,8960]{0,1:T(8,128)(2,1)} %bitcast.98, s32[128]{0:T(128)S(1)} %fusion.73, s32[48]{0:T(128)S(1)} %and_select_fusion), kind=kOutput, calls=%fused_computation.1 | convolution fusion | flops 110536704 | bytes 3154624 | tf_op jit(solution)/shard_map/dot_general | solution.py:576
  18.4 26.9 %scatter_pieces.1 = bf16[2,8,8960]{2,1,0:T(8,128)(2,1)} custom-call(bf16[6,8,8960]{2,1,0:T(8,128)(2,1)} %fusion.refs_0_), custom_call_target="tpu_custom_call" | custom-call | tf_op jit(solution)/shard_map/scatter_pieces/pallas_call | solution.py:446
  45.3 1.7 reshape.70
  47.1 0.8 constant_dynamic-slice_fusion.1
  47.8 0.4 fusion.21
  48.3 0.1 collective-permute-start
  48.4 0.5 collective-permute-start.1
  48.9 0.0 copy-done.3
  48.9 0.1 fusion.79
  49.0 1.4 collective-permute-start.2
  50.3 0.0 collective-permute-start.3
  50.3 1.8 pad.13.weight1
  52.2 0.0 collective-permute-done
  52.2 1.0 collective-permute-done.1
  53.2 0.7 fusion.29
  53.9 0.5 fusion.80
  54.4 0.0 copy-start.4
  54.4 0.0 copy-start.6
  54.4 0.2 pad_maximum_fusion.2
  54.6 0.7 copy-done.4
  55.4 0.3 copy-done.6
  55.6 0.8 fusion.78
  56.5 0.2 copy-done.15
  56.6 4.6 %multiply_convert_fusion = (bf16[10,512,256]{2,1,0:T(8,128)(2,1)S(1)}, f32[10,512,256]{2,1,0:T(8,128)}) fusion(bf16[720,256,1]{1,0,2:T(8,128)(2,1)S(1)} %bitcast.105, bf16[10,512,240]{1,2,0:T(8,128)(2,1)S(1)} %get-tuple-element.18, bf16[10,512,240]{1,2,0:T(8,128)(2,1)S(1)} %get-tuple-element.17, bf16[10,512,240]{1,2,0:T(8,128)(2,1)S(1)} %get-tuple-element.16), kind=kOutput, calls=%fused_computation.9 | convolution fusion | flops 1916108800 | bytes 15605760 | tf_op jit(solution)/shard_map/dot_general | solution.py:532
  61.2 3.6 %pad_slice_fusion.1 = (bf16[10,512,256]{2,1,0:T(8,128)(2,1)}, bf16[10,512,256]{2,1,0:T(8,128)(2,1)}) fusion(bf16[10,512,256]{2,1,0:T(8,128)(2,1)S(1)} %get-tuple-element.29), kind=kLoop, calls=%fused_computation.16 | loop fusion | bytes 7864320 | tf_op jit(solution)/shard_map/slice | solution.py:524
  64.9 0.0 collective-permute-done.2
  64.9 0.0 collective-permute-done.3
  64.9 1.9 pad_maximum_fusion.1.low.mid.high
  66.8 18.3 %backward_convs.1 = (bf16[10,512,256]{2,1,0:T(8,128)(2,1)}, bf16[8,512,80]{2,1,0:T(8,128)(2,1)}) custom-call(bf16[12,512,256]{2,1,0:T(8,128)(2,1)} %pad_maximum_fusion.1.low.mid.high, bf16[12,512,256]{2,1,0:T(8,128)(2,1)} %pad_maximum_fusion.1.low.mid.high, bf16[12,512,256]{2,1,0:T(8,128)(2,1)} %pad_maximum_fusion.1.low.mid.high, ...), custom_call_target="tpu_custom_call" | custom-call | flops 9059696640 | bytes 20971520 | tf_op jit(solution)/shard_map/backward_convs/pallas_call | solution.py:412
  85.0 2.5 %fusion.30 = bf16[2,8,112,80]{2,3,0,1:T(8,128)(2,1)} fusion(bf16[8,512,80]{2,1,0:T(8,128)(2,1)} %get-tuple-element.10, s32[2,112]{1,0:T(2,128)S(1)} %pad_add_fusion), kind=kOutput, calls=%fused_computation.47 | convolution fusion | flops 147058688 | bytes 942976 | tf_op jit(solution)/shard_map/nrb,arh->nabh/dot_general | solution.py:600
  87.5 1.2 copy.28
  88.7 1.2 reshape.73.refs_0_
  89.9 15.1 %gather_replies.1 = bf16[6,8,8960]{2,1,0:T(8,128)(2,1)} custom-call(bf16[2,8,8960]{2,1,0:T(8,128)(2,1)} %reshape.73.refs_0_), custom_call_target="tpu_custom_call" | custom-call | tf_op jit(solution)/shard_map/gather_replies/pallas_call | solution.py:468
  105.0 4.2 %fusion.59.refs_1_ = f32[8960,128]{1,0:T(8,128)} fusion(bf16[6,8,8960]{2,1,0:T(8,128)(2,1)} %gather_replies.1, s32[128]{0:T(128)S(1)} %fusion.73, s32[48]{0:T(128)S(1)} %and_select_fusion), kind=kOutput, calls=%fused_computation.58 | convolution fusion | flops 110106624 | bytes 5448384 | tf_op jit(solution)/shard_map/dot_general | solution.py:604
  109.3 0.0 copy-done.5
  109.3 0.0 copy-done.16
  109.3 1.3 fusion.55
  110.6 1.3 fusion.49
  112.0 1.3 fusion.43
  113.3 0.5 copy-done.10
  113.7 0.8 copy-done.11
  114.5 0.8 copy-done.12
  115.3 2.6 %fusion.23 = bf16[3072,256]{1,0:T(8,128)(2,1)} fusion(bf16[3072,256]{1,0:T(8,128)(2,1)} %fusion.43, bf16[8,512,256]{2,1,0:T(8,128)(2,1)S(1)} %copy-done.3, bf16[10,512,256]{2,1,0:T(8,128)(2,1)S(1)} %copy-done.12, bf16[10,512,256]{2,1,0:T(8,128)(2,1)S(1)} %copy-done.10, bf16[10,512,256]{2,1,0:T(8,128)(2,1)S(1)} %copy-done.11), kind=kOutput, calls=%fused_computation.39 | convolution fusion | flops 1634402304 | bytes 10354688 | tf_op jit(solution)/shard_map/dot_general | solution.py:544
  117.9 2.6 %fusion.25 = bf16[3072,256]{1,0:T(8,128)(2,1)} fusion(bf16[3072,256]{1,0:T(8,128)(2,1)} %fusion.23, bf16[8,512,256]{2,1,0:T(8,128)(2,1)S(1)} %copy-done.3, bf16[10,512,256]{2,1,0:T(8,128)(2,1)S(1)} %copy-done.12, bf16[10,512,256]{2,1,0:T(8,128)(2,1)S(1)} %copy-done.10, bf16[10,512,256]{2,1,0:T(8,128)(2,1)S(1)} %copy-done.11), kind=kOutput, calls=%fused_computation.41 | convolution fusion | flops 1634402304 | bytes 10354688 | tf_op jit(solution)/shard_map/dot_general | solution.py:544
  120.5 2.6 %fusion.27 = bf16[3072,256]{1,0:T(8,128)(2,1)} fusion(bf16[3072,256]{1,0:T(8,128)(2,1)} %fusion.25, bf16[8,512,256]{2,1,0:T(8,128)(2,1)S(1)} %copy-done.3, bf16[10,512,256]{2,1,0:T(8,128)(2,1)S(1)} %copy-done.12, bf16[10,512,256]{2,1,0:T(8,128)(2,1)S(1)} %copy-done.10, bf16[10,512,256]{2,1,0:T(8,128)(2,1)S(1)} %copy-done.11), kind=kOutput, calls=%fused_computation.43 | convolution fusion | flops 1634402304 | bytes 10354688 | tf_op jit(solution)/shard_map/dot_general | solution.py:544
  123.1 0.6 constant_dynamic-update-slice_fusion
  123.7 64.9 %sum_gradients.1 = (bf16[2,16,96,256]{3,2,1,0:T(8,128)(2,1)}, f32[112,32,128]{2,1,0:T(8,128)}, bf16[80,32,128]{2,1,0:T(8,128)(2,1)}) custom-call(bf16[2,16,96,256]{3,2,1,0:T(8,128)(2,1)} %bitcast.17.refs_0_, f32[8960,128]{1,0:T(8,128)} %fusion.59.refs_1_, f32[112,32,128]{2,1,0:T(8,128)} %get-tuple-element.15.refs_2_, bf16[80,32,128]{2,1,0:T(8,128)(2,1)} %bitcast.99, ...), custom_call_target="tpu_custom_call" | custom-call | tf_op jit(solution)/shard_map/sum_gradients/pallas_call | solution.py:492
  188.6 1.6 bitcast_convert_fusion
  190.3 1.6 slice.94
  191.8 0.9 slice.93
  192.7 1.2 copy.45
  194.0 0.8 copy.46
  (22 shorter events, 0.1 us)
Async XLA Ops:
  0.6 14.3 %copy-start = (s32[8,128]{1,0:T(8,128)S(1)}, s32[8,128]{1,0:T(8,128)}, u32[]{:S(2)}) copy-start(s32[8,128]{1,0:T(8,128)} %param.11) | copy-start | bytes 12292
  0.6 2.1 %copy-start.2 = (f32[1,112,32,128]{3,2,1,0:T(8,128)S(1)}, f32[1,112,32,128]{3,2,1,0:T(8,128)}, u32[]{:S(2)}) copy-start(f32[1,112,32,128]{3,2,1,0:T(8,128)} %param.8) | copy-start | bytes 5505028
  3.0 3.7 %copy-start.8 = (bf16[1,80,32,128]{3,2,1,0:T(8,128)(2,1)S(1)}, bf16[1,80,32,128]{3,2,1,0:T(8,128)(2,1)}, u32[]{:S(2)}) copy-start(bf16[1,80,32,128]{3,2,1,0:T(8,128)(2,1)} %param.9) | copy-start | bytes 1966084
  18.4 30.4 %copy-start.3 = (bf16[8,512,256]{2,1,0:T(8,128)(2,1)S(1)}, bf16[8,512,256]{2,1,0:T(8,128)(2,1)}, u32[]{:S(2)}) copy-start(bf16[8,512,256]{2,1,0:T(8,128)(2,1)} %param.15) | copy-start | bytes 6291460
  48.3 3.8 %collective-permute-start = (bf16[2,512,80]{1,2,0:T(8,128)(2,1)S(1)}, bf16[2,512,80]{1,2,0:T(8,128)(2,1)S(1)}, u32[]{:S(2)}, u32[]{:S(2)}) collective-permute-start(bf16[2,512,80]{1,2,0:T(8,128)(2,1)S(1)} %get-tuple-element.25), channel_id=1, source_target_pairs={{0,1},{1,2},{2,3},{3,4},{4,5},{5,6},{6,7},{7,8},{8,9},{9,10},{10,1... | collective-permute-start | bytes 491528 | tf_op jit(solution)/shard_map/ppermute | solution.py:17
  48.4 4.8 %collective-permute-start.1 = (bf16[2,512,80]{1,2,0:T(8,128)(2,1)S(1)}, bf16[2,512,80]{1,2,0:T(8,128)(2,1)S(1)}, u32[]{:S(2)}, u32[]{:S(2)}) collective-permute-start(bf16[2,512,80]{1,2,0:T(8,128)(2,1)S(1)} %get-tuple-element.26), channel_id=1, source_target_pairs={{1,0},{2,1},{3,2},{4,3},{5,4},{6,5},{7,6},{8,7},{9,8},{10,9},{11,1... | collective-permute-start | bytes 491528 | tf_op jit(solution)/shard_map/ppermute | solution.py:19
  49.0 15.9 %collective-permute-start.2 = (bf16[2,512,256]{2,1,0:T(8,128)(2,1)S(1)}, bf16[2,512,256]{2,1,0:T(8,128)(2,1)S(1)}, u32[]{:S(2)}, u32[]{:S(2)}) collective-permute-start(bf16[2,512,256]{2,1,0:T(8,128)(2,1)S(1)} %get-tuple-element.21), channel_id=1, source_target_pairs={{0,1},{1,2},{2,3},{3,4},{4,5},{5,6},{6,7},{7,8},{8,9},{9,10},{10,1... | collective-permute-start | bytes 1572872 | tf_op jit(solution)/shard_map/ppermute | solution.py:17
  50.3 14.6 %collective-permute-start.3 = (bf16[2,512,256]{2,1,0:T(8,128)(2,1)S(1)}, bf16[2,512,256]{2,1,0:T(8,128)(2,1)S(1)}, u32[]{:S(2)}, u32[]{:S(2)}) collective-permute-start(bf16[2,512,256]{2,1,0:T(8,128)(2,1)S(1)} %get-tuple-element.22), channel_id=1, source_target_pairs={{1,0},{2,1},{3,2},{4,3},{5,4},{6,5},{7,6},{8,7},{9,8},{10,9},{11,1... | collective-permute-start | bytes 1572872 | tf_op jit(solution)/shard_map/ppermute | solution.py:19
  54.4 1.0 copy-start.4
  54.4 1.3 copy-start.6
  55.6 1.0 copy-start.15
  61.2 3.6 %copy-start.9 = (bf16[10,512,256]{2,1,0:T(8,128)(2,1)}, bf16[10,512,256]{2,1,0:T(8,128)(2,1)S(1)}, u32[]{:S(2)}) copy-start(bf16[10,512,256]{2,1,0:T(8,128)(2,1)S(1)} %get-tuple-element.29) | copy-start | bytes 7864324
  105.0 4.3 %copy-start.5 = (bf16[12,512,80]{1,2,0:T(8,128)(2,1)S(1)}, bf16[12,512,80]{1,2,0:T(8,128)(2,1)}, u32[]{:S(2)}) copy-start(bf16[12,512,80]{1,2,0:T(8,128)(2,1)} %copy-done.4) | copy-start | bytes 2949124
  105.0 4.3 %copy-start.7 = (bf16[12,512,80]{1,2,0:T(8,128)(2,1)S(1)}, bf16[12,512,80]{1,2,0:T(8,128)(2,1)}, u32[]{:S(2)}) copy-start(bf16[12,512,80]{1,2,0:T(8,128)(2,1)} %copy-done.6) | copy-start | bytes 2949124
  105.0 4.3 %copy-start.16 = (bf16[10,512,256]{2,1,0:T(8,128)(2,1)S(1)}, bf16[10,512,256]{2,1,0:T(8,128)(2,1)}, u32[]{:S(2)}) copy-start(bf16[10,512,256]{2,1,0:T(8,128)(2,1)} %get-tuple-element.9) | copy-start | bytes 7864324
  111.9 1.8 copy-start.10
  111.9 2.6 %copy-start.11 = (bf16[10,512,256]{2,1,0:T(8,128)(2,1)S(1)}, bf16[10,512,256]{2,1,0:T(8,128)(2,1)}, u32[]{:S(2)}) copy-start(bf16[10,512,256]{2,1,0:T(8,128)(2,1)} %get-tuple-element.19) | copy-start | bytes 7864324
  111.9 3.4 %copy-start.12 = (bf16[10,512,256]{2,1,0:T(8,128)(2,1)S(1)}, bf16[10,512,256]{2,1,0:T(8,128)(2,1)}, u32[]{:S(2)}) copy-start(bf16[10,512,256]{2,1,0:T(8,128)(2,1)} %get-tuple-element.20) | copy-start | bytes 7864324
  190.3 2.5 %copy-start.13 = (f32[112,32,128]{2,1,0:T(8,128)S(1)}, f32[112,32,128]{2,1,0:T(8,128)}, u32[]{:S(2)}) copy-start(f32[112,32,128]{2,1,0:T(8,128)} %get-tuple-element.11) | copy-start | bytes 5505028
  191.8 2.1 %copy-start.14 = (bf16[80,32,128]{2,1,0:T(8,128)(2,1)S(1)}, bf16[80,32,128]{2,1,0:T(8,128)(2,1)}, u32[]{:S(2)}) copy-start(bf16[80,32,128]{2,1,0:T(8,128)(2,1)} %get-tuple-element.12) | copy-start | bytes 1966084
  191.8 3.0 %copy-start.1 = (s32[8,128]{1,0:T(8,128)S(1)}, s32[8,128]{1,0:T(8,128)}, u32[]{:S(2)}) copy-start(s32[8,128]{1,0:T(8,128)} %param.11) | copy-start | bytes 12292

commit v2 on v1

--- a/solution.py
+++ b/solution.py
@@ -117,89 +117,83 @@
             outgoing(part).wait_send()
 
 
-def reply_kernel(blocks, bands, replies, gathered, send_sems, recv_sems):
+def reply_kernel(blocks, bands, replies, gathered, send_sems, recv_sems, hand_sems):
     me = lax.axis_index("blk")
     band = me % bands
+    core = me % 2
     first = me - band
+    partner = me + 1 - 2 * core
     before = (first + blocks - bands) % blocks
     after = (first + bands) % blocks
     edge = jnp.logical_or(band == 0, band == bands - 1)
+    own = band + 1
+    order = list(range(1, bands + 1)) + [0, bands + 1]
     barrier = pltpu.get_barrier_semaphore()
-    greet(barrier, (first + blocks - 1) % blocks)
-    greet(barrier, after)
-    for other in range(bands):
-        @pl.when(band != other)
-        def _():
-            greet(barrier, first + other)
+    greet(barrier, partner)
+    for part in order:
+        @pl.when(jnp.logical_and((part + 1) % 2 == core, part != own))
+        def _():
+            greet(barrier, (first + blocks - 1 + part) % blocks)
 
     @pl.when(edge)
     def _():
-        pl.semaphore_wait(barrier, 2 * bands - 1)
+        pl.semaphore_wait(barrier, bands)
 
     @pl.when(jnp.logical_not(edge))
     def _():
-        pl.semaphore_wait(barrier, bands - 1)
-
-    def near(other):
+        pl.semaphore_wait(barrier, bands // 2)
+
+    def move(source, part, sem, target):
         return remote(
-            replies.at[0],
-            gathered.at[band + 1],
-            send_sems.at[other],
-            recv_sems.at[band + 1],
-            first + other,
-        )
-
-    def far_after(other):
-        return remote(
-            replies.at[1],
-            gathered.at[0],
-            send_sems.at[bands + other],
-            recv_sems.at[0],
-            after + other,
-        )
-
-    def far_before(other):
-        return remote(
-            replies.at[1],
-            gathered.at[bands + 1],
-            send_sems.at[bands + other],
-            recv_sems.at[bands + 1],
-            before + other,
-        )
+            replies.at[source], gathered.at[part], send_sems.at[sem], recv_sems.at[part], target
+        )
+
+    def sends(action):
+        for other in range(bands):
+            alike = other % 2 == core
+
+            @pl.when(jnp.logical_and(alike, band != other))
+            def _():
+                action(move(0, own, other, first + other))
+
+            @pl.when(jnp.logical_and(alike, band == 0))
+            def _():
+                action(move(1, bands + 1, bands + other, before + other))
+
+            @pl.when(jnp.logical_and(alike, band == bands - 1))
+            def _():
+                action(move(1, 0, bands + other, after + other))
+
+    def handing(part):
+        block = gathered.at[part]
+        return remote(block, block, hand_sems.at[part], recv_sems.at[part], partner)
 
     def arriving(part):
         return remote(
-            replies.at[0], gathered.at[part], send_sems.at[0], recv_sems.at[part], first
-        )
-
-    for other in range(bands):
-        @pl.when(band == 0)
-        def _():
-            far_before(other).start()
-
-        @pl.when(band == bands - 1)
-        def _():
-            far_after(other).start()
-
-        @pl.when(band != other)
-        def _():
-            near(other).start()
-    gathered[pl.ds(band + 1, 1)] = replies[pl.ds(0, 1)]
-    for part in (0, bands + 1):
-        arriving(part).wait_recv()
-    for other in range(bands):
-        @pl.when(band != other)
-        def _():
-            arriving(other + 1).wait_recv()
-            near(other).wait_send()
-
-        @pl.when(band == 0)
-        def _():
-            far_before(other).wait_send()
-
-        @pl.when(band == bands - 1)
-        def _():
-            far_after(other).wait_send()
+            replies.at[0], gathered.at[part], send_sems.at[0], recv_sems.at[part], partner
+        )
+
+    given = remote(
+        replies.at[0], gathered.at[own], hand_sems.at[own], recv_sems.at[own], partner
+    )
+    sends(lambda copy: copy.start())
+    given.start()
+    gathered[pl.ds(own, 1)] = replies[pl.ds(0, 1)]
+    for part in order:
+        @pl.when(jnp.logical_and((part + 1) % 2 == core, part != own))
+        def _():
+            arriving(part).wait_recv()
+            handing(part).start()
+    for part in order:
+        @pl.when((part + 1) % 2 != core)
+        def _():
+            arriving(part).wait_recv()
+
+        @pl.when(jnp.logical_and((part + 1) % 2 == core, part != own))
+        def _():
+            handing(part).wait_send()
+    given.wait_send()
+    sends(lambda copy: copy.wait_send())
 
 
 def context_part(wide, probs, grad, start, count):
@@ -255,91 +249,105 @@
 
 
 def sum_kernel(
-    chips, terms, wide, probs, context, lidar, out, logit_grad, context_grad,
-    features, mean, pair, local, stage_r, stage_l, land_r, land_l,
-    pair_sems, ring_r, ring_l, pass_r, pass_l,
+    chips, terms, wide, probs, context, lidar, first_grad, second_grad, logit_grad,
+    context_grad, features, mean, pair, local, out, chain_from, own_from, chain_to, own_to,
+    pair_sems, chain_sems, own_sems, near_sems, far_sems,
 ):
     me = lax.axis_index("blk")
     core = me % 2
     chip = me // 2
     blocks = 2 * chips
     partner = me + 1 - 2 * core
-    right = (me + 2) % blocks
-    left = (me + blocks - 2) % blocks
-    rights = chips // 2
-    lefts = chips - 1 - rights
+    ways = ((0, 1, chips // 2), (1, -1, chips - 1 - chips // 2))
+    rounds = chips // 4
+    kind = terms.dtype
+
+    def place(step):
+        return (chip + step + chips) % chips
+
+    def device(step):
+        return (me + 2 * step + blocks) % blocks
+
     barrier = pltpu.get_barrier_semaphore()
-    for other in (partner, right, left):
+    for other in (partner, device(1), device(-1), device(2), device(-2)):
         greet(barrier, other)
-    pl.semaphore_wait(barrier, 3)
+    pl.semaphore_wait(barrier, 5)
     swap = remote(terms.at[1 - core], pair, pair_sems.at[0], pair_sems.at[1], partner)
     swap.start()
     features[...] = context[...].astype(jnp.float32)
     mean[...] = jnp.zeros_like(mean)
-    parts = 2 * rights
+    parts = 4 * rounds
     depths = probs.shape[0] // parts
     widths = context.shape[0] // parts
     swap.wait_recv()
     local[...] = (
         terms[pl.ds(core, 1)][0].astype(jnp.float32) + pair[...].astype(jnp.float32)
     )
-    moves_r = []
-    moves_l = []
-    for step in range(rights):
-        chunk = (chip + rights - step) % chips
-        value = local[pl.ds(chunk, 1)][0]
-        if step:
-            moves_r[-1].wait_recv()
-            value = value + land_r[step - 1].astype(jnp.float32)
-        stage_r[step] = value.astype(stage_r.dtype)
-        move = remote(
-            stage_r.at[step], land_r.at[step], ring_r.at[0, step], ring_r.at[1, step], right
-        )
-        move.start()
-        moves_r.append(move)
-        if step < lefts:
-            chunk = (chip + chips - lefts + step) % chips
-            value = local[pl.ds(chunk, 1)][0]
-            if step:
-                moves_l[-1].wait_recv()
-                value = value + land_l[step - 1].astype(jnp.float32)
-            stage_l[step] = value.astype(stage_l.dtype)
-            move = remote(
-                stage_l.at[step], land_l.at[step], ring_l.at[0, step], ring_l.at[1, step], left
-            )
-            move.start()
-            moves_l.append(move)
-        for part in (2 * step, 2 * step + 1):
+
+    def mine(step):
+        return local[pl.ds(place(step), 1)][0]
+
+    def chain_move(way, sign, reach, index):
+        hop = 2 if reach - 2 * index >= 2 else 1
+        return remote(
+            chain_from.at[way, index], chain_to.at[way, index],
+            chain_sems.at[way, 0, index], chain_sems.at[way, 1, index], device(sign * hop),
+        )
+
+    def own_move(way, sign, index):
+        return remote(
+            own_from.at[way, index], own_to.at[way, index],
+            own_sems.at[way, 0, index], own_sems.at[way, 1, index], device(sign),
+        )
+
+    for index in range(rounds):
+        for way, sign, reach in ways:
+            value = mine(sign * (reach - 2 * index))
+            if index:
+                chain_move(way, sign, reach, index - 1).wait_recv()
+                own_move(way, sign, index - 1).wait_recv()
+                value = value + chain_to[way, index - 1].astype(jnp.float32)
+                value = value + own_to[way, index - 1].astype(jnp.float32)
+            chain_from[way, index] = value.astype(kind)
+            chain_move(way, sign, reach, index).start()
+        for way, sign, reach in ways:
+            if index < reach // 2:
+                own_from[way, index] = mine(sign * (reach - 1 - 2 * index)).astype(kind)
+                own_move(way, sign, index).start()
+        for part in range(4 * index, 4 * index + 4):
             context_part(wide, probs, context_grad, part * widths, widths)
-    moves_l[-1].wait_recv()
-    moves_r[-1].wait_recv()
-    total = (
-        local[pl.ds(chip, 1)][0]
-        + land_r[rights - 1].astype(jnp.float32)
-        + land_l[lefts - 1].astype(jnp.float32)
-    )
-    out[pl.ds(core, 1), pl.ds(chip, 1)] = total.astype(out.dtype)[None, None]
-
-    def passing_r(step, origin):
-        block = out.at[core, (origin + chips - step) % chips]
-        return remote(block, block, pass_r.at[0, step], pass_r.at[1, step], right)
-
-    def passing_l(step, origin):
-        block = out.at[core, (origin + step) % chips]
-        return remote(block, block, pass_l.at[0, step], pass_l.at[1, step], left)
-
-    for step in range(rights):
-        if step:
-            passing_r(step - 1, chip + chips - 1).wait_recv()
-        passing_r(step, chip).start()
-        if step < lefts:
-            if step:
-                passing_l(step - 1, chip + 1).wait_recv()
-            passing_l(step, chip).start()
-        for part in (2 * step, 2 * step + 1):
+    total = mine(0)
+    for way, sign, reach in ways:
+        chain_move(way, sign, reach, rounds - 1).wait_recv()
+        total = total + chain_to[way, rounds - 1].astype(jnp.float32)
+        if rounds == reach // 2:
+            own_move(way, sign, rounds - 1).wait_recv()
+            total = total + own_to[way, rounds - 1].astype(jnp.float32)
+    out[pl.ds(core, 1), pl.ds(chip, 1)] = total.astype(kind)[None, None]
+
+    def passing(way, sign, index, hop, origin):
+        block = out.at[core, (chip + origin - 2 * sign * index + 2 * chips) % chips]
+        sems = near_sems if hop == 1 else far_sems
+        return remote(
+            block, block, sems.at[way, 0, index], sems.at[way, 1, index], device(sign * hop)
+        )
+
+    def hops(reach, index):
+        return [hop for hop in (2, 1) if 2 * index + hop <= reach]
+
+    for index in range(rounds):
+        for way, sign, reach in ways:
+            if index:
+                passing(way, sign, index - 1, 2, -2 * sign).wait_recv()
+            for hop in hops(reach, index):
+                passing(way, sign, index, hop, 0).start()
+        for part in range(4 * index, 4 * index + 4):
             prob_part(wide, features, probs, logit_grad, mean, part * depths, depths)
-    passing_l(lefts - 1, chip + 1).wait_recv()
-    passing_r(rights - 1, chip + chips - 1).wait_recv()
+    for way, sign, reach in ways:
+        for index in range(rounds):
+            passing(way, sign, index, 1, -sign).wait_recv()
+        if 2 in hops(reach, rounds - 1):
+            passing(way, sign, rounds - 1, 2, -2 * sign).wait_recv()
     whole = remote(
         out.at[core], out.at[core], pair_sems.at[2], pair_sems.at[3], partner
     )
@@ -348,14 +356,28 @@
     remote(
         out.at[1 - core], out.at[1 - core], pair_sems.at[2], pair_sems.at[3], partner
     ).wait_recv()
+    height = terms.shape[2]
+    split = first_grad.shape[0]
+    final = split + second_grad.shape[0]
+    for half in range(2):
+        for chunk in range(chips):
+            low = (half * chips + chunk) * height
+            block = out[half, chunk].astype(jnp.float32)
+            cut = min(max(split - low, 0), height)
+            end = min(final - low, height)
+            if cut > 0:
+                first_grad[low : low + cut] = block[:cut]
+            if end > cut:
+                second_grad[low + cut - split : low + end - split] = block[cut:end]
     whole.wait_send()
     swap.wait_send()
-    for move in moves_r + moves_l:
-        move.wait_send()
-    for step in range(rights):
-        passing_r(step, chip).wait_send()
-    for step in range(lefts):
-        passing_l(step, chip).wait_send()
+    for way, sign, reach in ways:
+        for index in range(rounds):
+            chain_move(way, sign, reach, index).wait_send()
+            if index < reach // 2:
+                own_move(way, sign, index).wait_send()
+            for hop in hops(reach, index):
+                passing(way, sign, index, hop, 0).wait_send()
 
 
 def slid(field, step):
@@ -473,16 +495,16 @@
         scratch_shapes=[
             pltpu.SemaphoreType.DMA((2 * bands,)),
             pltpu.SemaphoreType.DMA((bands + 2,)),
+            pltpu.SemaphoreType.DMA((bands + 2,)),
         ],
         compiler_params=pltpu.CompilerParams(collective_id=1, has_side_effects=True),
         name="gather_replies",
     )(replies)
 
 
-def summed(terms, wide, probs, context, lidar):
+def summed(terms, wide, probs, context, lidar, rows1, rows2):
     chips = terms.shape[1]
-    rights = chips // 2
-    lefts = chips - 1 - rights
+    rounds = chips // 4
     block = terms.shape[2:]
     kind = terms.dtype
 
@@ -492,27 +514,23 @@
     return pl.pallas_call(
         kernel,
         out_shape=(
-            jax.ShapeDtypeStruct(terms.shape, kind),
+            jax.ShapeDtypeStruct((rows1,) + block[1:], jnp.float32),
+            jax.ShapeDtypeStruct((rows2,) + block[1:], jnp.float32),
             jax.ShapeDtypeStruct(probs.shape, jnp.float32),
             jax.ShapeDtypeStruct(context.shape, context.dtype),
         ),
         in_specs=[VMEM] * 5,
-        out_specs=(VMEM,) * 3,
+        out_specs=(VMEM,) * 4,
         scratch_shapes=[
             pltpu.VMEM(context.shape, jnp.float32),
             pltpu.VMEM(probs.shape[1:], jnp.float32),
             pltpu.VMEM((chips,) + block, kind),
             pltpu.VMEM((chips,) + block, jnp.float32),
-            pltpu.VMEM((rights,) + block, kind),
-            pltpu.VMEM((lefts,) + block, kind),
-            pltpu.VMEM((rights,) + block, kind),
-            pltpu.VMEM((lefts,) + block, kind),
-            pltpu.SemaphoreType.DMA((4,)),
-            pltpu.SemaphoreType.DMA((2, rights)),
-            pltpu.SemaphoreType.DMA((2, lefts)),
-            pltpu.SemaphoreType.DMA((2, rights)),
-            pltpu.SemaphoreType.DMA((2, lefts)),
-        ],
+            pltpu.VMEM((2, chips) + block, kind),
+        ]
+        + [pltpu.VMEM((2, rounds) + block, kind)] * 4
+        + [pltpu.SemaphoreType.DMA((4,))]
+        + [pltpu.SemaphoreType.DMA((2, 2, rounds))] * 4,
         compiler_params=pltpu.CompilerParams(collective_id=2, has_side_effects=True),
         name="sum_gradients",
     )(terms, wide, probs, context, lidar)
@@ -614,19 +632,20 @@
     terms = jnp.concatenate(
         [conv1_grad, conv2_grad, jnp.zeros((padding, hidden_width), jnp.bfloat16)], axis=0
     )
-    terms, logit_grad, context_grad = summed(
+    first_grad, second_grad, logit_grad, context_grad = summed(
         terms.reshape(2, blocks // 2, -1, hidden_width),
         wide,
         depth_prob,
         view_context,
         lidar_bins[0],
-    )
-    terms = terms.reshape(-1, hidden_width).astype(jnp.float32)
+        rows1,
+        rows2,
+    )
     return (
         logit_grad[None],
         context_grad[None],
-        terms[:rows1].reshape(3, 3, channels, hidden_width),
-        terms[rows1 : rows1 + rows2].reshape(3, 3, hidden_width, hidden_width),
+        first_grad.reshape(3, 3, channels, hidden_width),
+        second_grad.reshape(3, 3, hidden_width, hidden_width),
     )
 
 

time: 195 us -> 178 us (0.913)
  Pallas kernels: 125 us -> 108 us
    pallas_call x1, Pallas kernels: 64.9 us -> 51.5 us  [summed(): pl.pallas_call(kernel, out_shape=(jax.ShapeDtypeStruct((rows1,) + block[1...]
    unnamed x36 -> x40, local copies, waits for them, and re-layouts: 5.5 us -> 9.59 us
    pallas_call x1, Pallas kernels: 15.1 us -> 11.3 us  [gather_replies(): pl.pallas_call(kernel, out_shape=jax.ShapeDtypeStruct((bands + 2,) + shap...]
    slice x2 -> x0, local copies, waits for them, and re-layouts: 2.47 us -> none  [the longest x1 1.56 us: shards(): terms[rows1:rows1 + rows2].reshape(3, 3, hidden_width, hidden_width)]
  transfers between devices with their start and end apart: 4 -> 4, of which waited for: 1 -> 1; matrix products, arithmetic and copies ran while one was open for 6% -> 7% of each run, Pallas kernels for 0% -> 0%
where the time goes in v2:
time: 178 us
  Pallas kernels  108 us (61%)
  local copies, waits for them, and re-layouts  29.8 us (17%)
  matrix products  29.5 us (17%)
  other arithmetic  6.57 us (4%)
  starting transfers between devices  1.91 us (1%)
    pallas_call x1, Pallas kernels, summed(): pl.pallas_call(kernel, out_shape=(jax.ShapeDtypeStruct((rows1,) + block[1...  51.5 us
    pallas_call x1, Pallas kernels, scatter_pieces(): pl.pallas_call(kernel, out_shape=jax.ShapeDtypeStruct((2,) + shape, piece...  26.9 us
    pallas_call x1, Pallas kernels, backward(): pl.pallas_call(back_kernel, grid=(height,), out_shape=(jax.ShapeDtypeStru...  18.3 us
    dot_general x6, matrix products, weight_grad(): lax.dot_general(left, flat, (((0,), (0,)), ((), ())), preferred_element_t...  11.8 us
    pallas_call x1, Pallas kernels, gather_replies(): pl.pallas_call(kernel, out_shape=jax.ShapeDtypeStruct((bands + 2,) + shap...  11.3 us
    unnamed x40, local copies, waits for them, and re-layouts  9.59 us
    dot_general x1, matrix products, conv_rows(): jnp.dot(flat, weight.reshape(-1, weight.shape[3]), preferred_element_type...  4.6 us
    dot_general x1, matrix products, shards(): lax.dot_general(gathered.reshape(span, bin_count * channels), column_hot,...  4.24 us
  transfers between devices with their start and end apart: 4, of which 1 were waited for; matrix products, arithmetic and copies ran while one was open for 7% of the time, Pallas kernels for 0%

profile of v2, /device:TPU:69, one launch (start us, length us, event | category | flops | bytes accessed | tf_op | source)
XLA Modules:
  0.0 177.7 jit_solution(14504520274203217442)
XLA Ops:
  0.6 0.0 copy-start
  0.6 0.0 copy-start.2
  0.7 1.8 %reduce_max.9 = f32[32,128]{1,0:T(8,128)S(1)} reduce(f32[1,112,32,128]{3,2,1,0:T(8,128)} %param.8, f32[]{:T(128)} %constant.68.clone.1), dimensions={0,1}, to_apply=%region_0.1 | reduce | flops 454656 | bytes 1851396 | tf_op jit(solution)/shard_map/reduce_max | solution.py:583
  2.5 0.2 copy-done.2
  2.7 0.3 fusion.10
  3.0 1.6 fusion.76
  4.6 2.1 %copy.20 = bf16[112,32,128]{0,1,2:T(8,128)(2,1)} copy(bf16[112,32,128]{2,1,0:T(8,128)(2,1)S(1)} %get-tuple-element.16) | data formatting | bytes 1835008 | tf_op jit(solution)/shard_map/convert_element_type | solution.py:584
  6.8 0.0 copy-done.8
  6.8 1.9 %copy.21 = bf16[80,32,128]{0,1,2:T(8,128)(2,1)} copy(bf16[80,32,128]{2,1,0:T(8,128)(2,1)S(1)} %bitcast.97) | data formatting | bytes 1310720 | tf_op jit(solution)/shard_map/squeeze | solution.py:585
  8.7 2.4 %convolution_convert_fusion.1 = bf16[128,112,80]{1,2,0:T(8,128)(2,1)S(1)} fusion(bf16[112,32,128]{0,1,2:T(8,128)(2,1)} %copy.20, bf16[80,32,128]{0,1,2:T(8,128)(2,1)} %copy.21), kind=kOutput, calls=%fused_computation.17 | convolution fusion | flops 74547200 | bytes 3866624 | tf_op jit(solution)/shard_map/brc,hrc->cbh/dot_general | solution.py:586
  11.1 3.8 %copy.22 = bf16[128,112,80]{0,2,1:T(8,128)(2,1)} copy(bf16[128,112,80]{1,2,0:T(8,128)(2,1)S(1)} %convolution_convert_fusion.1) | data formatting | bytes 4587520 | tf_op jit(solution)/shard_map/convert_element_type | solution.py:587
  14.9 0.0 copy-done
  14.9 3.5 %fusion.refs_0_ = bf16[6,8,8960]{2,1,0:T(8,128)(2,1)} fusion(bf16[128,8960]{0,1:T(8,128)(2,1)} %bitcast.95, s32[128]{0:T(128)S(1)} %fusion.73, s32[48]{0:T(128)S(1)} %and_select_fusion), kind=kOutput, calls=%fused_computation.1 | convolution fusion | flops 110536704 | bytes 3154624 | tf_op jit(solution)/shard_map/dot_general | solution.py:594
  18.4 26.9 %scatter_pieces.1 = bf16[2,8,8960]{2,1,0:T(8,128)(2,1)} custom-call(bf16[6,8,8960]{2,1,0:T(8,128)(2,1)} %fusion.refs_0_), custom_call_target="tpu_custom_call" | custom-call | tf_op jit(solution)/shard_map/scatter_pieces/pallas_call | solution.py:468
  45.3 1.7 reshape.67
  47.1 0.8 constant_dynamic-slice_fusion.1
  47.9 0.4 fusion.21
  48.3 0.1 collective-permute-start
  48.4 0.5 collective-permute-start.1
  48.9 0.0 copy-done.3
  48.9 0.1 fusion.79
  49.0 1.4 collective-permute-start.2
  50.3 0.0 collective-permute-start.3
  50.3 1.8 %pad.13.weight1 = bf16[3,3,128,256]{3,2,1,0:T(8,128)(2,1)} pad(bf16[3,3,80,256]{3,2,1,0:T(8,128)(2,1)} %param.13, bf16[]{:T(256)} %constant.71.clone.1), padding=0_0x0_0x0_48x0_0 | pad | bytes 958466 | tf_op jit(solution)/shard_map/jit(_pad)/pad | solution.py:426
  52.2 0.0 collective-permute-done
  52.2 1.0 collective-permute-done.1
  53.2 0.7 fusion.29
  53.9 0.5 fusion.80
  54.4 0.0 copy-start.4
  54.4 0.0 copy-start.6
  54.4 0.2 pad_maximum_fusion.2
  54.7 0.7 copy-done.4
  55.4 0.3 copy-done.6
  55.7 0.8 fusion.78
  56.5 0.2 copy-done.16
  56.6 4.6 %multiply_convert_fusion = (bf16[10,512,256]{2,1,0:T(8,128)(2,1)S(1)}, f32[10,512,256]{2,1,0:T(8,128)}) fusion(bf16[720,256,1]{1,0,2:T(8,128)(2,1)S(1)} %bitcast.102, bf16[10,512,240]{1,2,0:T(8,128)(2,1)S(1)} %get-tuple-element.20, bf16[10,512,240]{1,2,0:T(8,128)(2,1)S(1)} %get-tuple-element.19, bf16[10,512,240]{1,2,0:T(8,128)(2,1)S(1)} %get-tuple-element.18), kind=kOutput, calls=%fused_computation.9 | convolution fusion | flops 1916108800 | bytes 15605760 | tf_op jit(solution)/shard_map/dot_general | solution.py:550
  61.2 3.6 %pad_slice_fusion.1 = (bf16[10,512,256]{2,1,0:T(8,128)(2,1)}, bf16[10,512,256]{2,1,0:T(8,128)(2,1)}) fusion(bf16[10,512,256]{2,1,0:T(8,128)(2,1)S(1)} %get-tuple-element.31), kind=kLoop, calls=%fused_computation.16 | loop fusion | bytes 7864320 | tf_op jit(solution)/shard_map/slice | solution.py:542
  64.9 0.0 copy-done.9
  64.9 0.0 collective-permute-done.2
  64.9 0.0 collective-permute-done.3
  64.9 1.9 %pad_maximum_fusion.1.low.mid.high = bf16[12,512,256]{2,1,0:T(8,128)(2,1)} fusion(bf16[2,512,256]{2,1,0:T(8,128)(2,1)S(1)} %collective-permute-done.3, bf16[8,512,256]{2,1,0:T(8,128)(2,1)S(1)} %copy-done.3, bf16[2,512,256]{2,1,0:T(8,128)(2,1)S(1)} %collective-permute-done.2), kind=kLoop, calls=%fused_computation.12 | loop fusion | flops 3145728 | bytes 6291456 | tf_op jit(solution)/shard_map/concatenate | solution.py:15
  66.8 18.3 %backward_convs.1 = (bf16[10,512,256]{2,1,0:T(8,128)(2,1)}, bf16[8,512,80]{2,1,0:T(8,128)(2,1)}) custom-call(bf16[12,512,256]{2,1,0:T(8,128)(2,1)} %pad_maximum_fusion.1.low.mid.high, bf16[12,512,256]{2,1,0:T(8,128)(2,1)} %pad_maximum_fusion.1.low.mid.high, bf16[12,512,256]{2,1,0:T(8,128)(2,1)} %pad_maximum_fusion.1.low.mid.high, ...), custom_call_target="tpu_custom_call" | custom-call | flops 9059696640 | bytes 20971520 | tf_op jit(solution)/shard_map/backward_convs/pallas_call | solution.py:434
  85.1 2.5 %fusion.30 = bf16[2,8,112,80]{2,3,0,1:T(8,128)(2,1)} fusion(bf16[8,512,80]{2,1,0:T(8,128)(2,1)} %get-tuple-element.11, s32[2,112]{1,0:T(2,128)S(1)} %pad_add_fusion), kind=kOutput, calls=%fused_computation.46 | convolution fusion | flops 147058688 | bytes 942976 | tf_op jit(solution)/shard_map/nrb,arh->nabh/dot_general | solution.py:618
  87.6 1.2 copy.28
  88.8 1.2 reshape.70.refs_0_
  90.0 11.3 %gather_replies.1 = bf16[6,8,8960]{2,1,0:T(8,128)(2,1)} custom-call(bf16[2,8,8960]{2,1,0:T(8,128)(2,1)} %reshape.70.refs_0_), custom_call_target="tpu_custom_call" | custom-call | tf_op jit(solution)/shard_map/gather_replies/pallas_call | solution.py:490
  101.3 4.2 %fusion.59.refs_1_ = f32[8960,128]{1,0:T(8,128)} fusion(bf16[6,8,8960]{2,1,0:T(8,128)(2,1)} %gather_replies.1, s32[128]{0:T(128)S(1)} %fusion.73, s32[48]{0:T(128)S(1)} %and_select_fusion), kind=kOutput, calls=%fused_computation.57 | convolution fusion | flops 110106624 | bytes 5448384 | tf_op jit(solution)/shard_map/dot_general | solution.py:622
  105.6 0.0 copy-done.17
  105.6 1.3 fusion.55
  106.9 1.3 fusion.49
  108.2 1.3 fusion.43
  109.6 0.5 copy-done.10
  110.0 0.8 copy-done.11
  110.8 0.8 copy-done.12
  111.6 2.6 %fusion.23 = bf16[3072,256]{1,0:T(8,128)(2,1)} fusion(bf16[3072,256]{1,0:T(8,128)(2,1)} %fusion.43, bf16[8,512,256]{2,1,0:T(8,128)(2,1)S(1)} %copy-done.3, bf16[10,512,256]{2,1,0:T(8,128)(2,1)S(1)} %copy-done.12, bf16[10,512,256]{2,1,0:T(8,128)(2,1)S(1)} %copy-done.10, bf16[10,512,256]{2,1,0:T(8,128)(2,1)S(1)} %copy-done.11), kind=kOutput, calls=%fused_computation.38 | convolution fusion | flops 1634402304 | bytes 10354688 | tf_op jit(solution)/shard_map/dot_general | solution.py:562
  114.2 2.6 %fusion.25 = bf16[3072,256]{1,0:T(8,128)(2,1)} fusion(bf16[3072,256]{1,0:T(8,128)(2,1)} %fusion.23, bf16[8,512,256]{2,1,0:T(8,128)(2,1)S(1)} %copy-done.3, bf16[10,512,256]{2,1,0:T(8,128)(2,1)S(1)} %copy-done.12, bf16[10,512,256]{2,1,0:T(8,128)(2,1)S(1)} %copy-done.10, bf16[10,512,256]{2,1,0:T(8,128)(2,1)S(1)} %copy-done.11), kind=kOutput, calls=%fused_computation.40 | convolution fusion | flops 1634402304 | bytes 10354688 | tf_op jit(solution)/shard_map/dot_general | solution.py:562
  116.8 2.6 %fusion.27 = bf16[3072,256]{1,0:T(8,128)(2,1)} fusion(bf16[3072,256]{1,0:T(8,128)(2,1)} %fusion.25, bf16[8,512,256]{2,1,0:T(8,128)(2,1)S(1)} %copy-done.3, bf16[10,512,256]{2,1,0:T(8,128)(2,1)S(1)} %copy-done.12, bf16[10,512,256]{2,1,0:T(8,128)(2,1)S(1)} %copy-done.10, bf16[10,512,256]{2,1,0:T(8,128)(2,1)S(1)} %copy-done.11), kind=kOutput, calls=%fused_computation.42 | convolution fusion | flops 1634402304 | bytes 10354688 | tf_op jit(solution)/shard_map/dot_general | solution.py:562
  119.4 0.6 constant_dynamic-update-slice_fusion
  120.0 51.5 %sum_gradients.1 = (f32[720,256]{1,0:T(8,128)}, f32[2304,256]{1,0:T(8,128)}, f32[112,32,128]{2,1,0:T(8,128)}, bf16[80,32,128]{2,1,0:T(8,128)(2,1)}) custom-call(bf16[2,16,96,256]{3,2,1,0:T(8,128)(2,1)} %bitcast.17.refs_0_, f32[8960,128]{1,0:T(8,128)} %fusion.59.refs_1_, f32[112,32,128]{2,1,0:T(8,128)} %get-tuple-element.17.refs_2_, ...), custom_call_target="tpu_custom_call" | custom-call | tf_op jit(solution)/shard_map/sum_gradients/pallas_call | solution.py:514
  171.5 3.0 %copy.47 = f32[1,112,32,128]{3,2,1,0:T(8,128)} copy(f32[1,112,32,128]{3,2,1,0:T(8,128)} %bitcast.99) | data formatting | bytes 3670016
  174.6 0.0 copy-done.15
  174.6 0.8 copy.48
  175.4 0.9 copy.49
  176.3 1.4 copy.50
  (23 shorter events, 0.1 us)
Async XLA Ops:
  0.6 14.3 %copy-start = (s32[8,128]{1,0:T(8,128)S(1)}, s32[8,128]{1,0:T(8,128)}, u32[]{:S(2)}) copy-start(s32[8,128]{1,0:T(8,128)} %param.11) | copy-start | bytes 12292
  0.6 2.1 %copy-start.2 = (f32[1,112,32,128]{3,2,1,0:T(8,128)S(1)}, f32[1,112,32,128]{3,2,1,0:T(8,128)}, u32[]{:S(2)}) copy-start(f32[1,112,32,128]{3,2,1,0:T(8,128)} %param.8) | copy-start | bytes 5505028
  3.0 3.7 %copy-start.8 = (bf16[1,80,32,128]{3,2,1,0:T(8,128)(2,1)S(1)}, bf16[1,80,32,128]{3,2,1,0:T(8,128)(2,1)}, u32[]{:S(2)}) copy-start(bf16[1,80,32,128]{3,2,1,0:T(8,128)(2,1)} %param.9) | copy-start | bytes 1966084
  18.4 30.5 %copy-start.3 = (bf16[8,512,256]{2,1,0:T(8,128)(2,1)S(1)}, bf16[8,512,256]{2,1,0:T(8,128)(2,1)}, u32[]{:S(2)}) copy-start(bf16[8,512,256]{2,1,0:T(8,128)(2,1)} %param.15) | copy-start | bytes 6291460
  48.3 3.8 %collective-permute-start = (bf16[2,512,80]{1,2,0:T(8,128)(2,1)S(1)}, bf16[2,512,80]{1,2,0:T(8,128)(2,1)S(1)}, u32[]{:S(2)}, u32[]{:S(2)}) collective-permute-start(bf16[2,512,80]{1,2,0:T(8,128)(2,1)S(1)} %get-tuple-element.27), channel_id=1, source_target_pairs={{0,1},{1,2},{2,3},{3,4},{4,5},{5,6},{6,7},{7,8},{8,9},{9,10},{10,1... | collective-permute-start | bytes 491528 | tf_op jit(solution)/shard_map/ppermute | solution.py:17
  48.4 4.8 %collective-permute-start.1 = (bf16[2,512,80]{1,2,0:T(8,128)(2,1)S(1)}, bf16[2,512,80]{1,2,0:T(8,128)(2,1)S(1)}, u32[]{:S(2)}, u32[]{:S(2)}) collective-permute-start(bf16[2,512,80]{1,2,0:T(8,128)(2,1)S(1)} %get-tuple-element.28), channel_id=1, source_target_pairs={{1,0},{2,1},{3,2},{4,3},{5,4},{6,5},{7,6},{8,7},{9,8},{10,9},{11,1... | collective-permute-start | bytes 491528 | tf_op jit(solution)/shard_map/ppermute | solution.py:19
  49.0 15.9 %collective-permute-start.2 = (bf16[2,512,256]{2,1,0:T(8,128)(2,1)S(1)}, bf16[2,512,256]{2,1,0:T(8,128)(2,1)S(1)}, u32[]{:S(2)}, u32[]{:S(2)}) collective-permute-start(bf16[2,512,256]{2,1,0:T(8,128)(2,1)S(1)} %get-tuple-element.23), channel_id=1, source_target_pairs={{0,1},{1,2},{2,3},{3,4},{4,5},{5,6},{6,7},{7,8},{8,9},{9,10},{10,1... | collective-permute-start | bytes 1572872 | tf_op jit(solution)/shard_map/ppermute | solution.py:17
  50.3 14.5 %collective-permute-start.3 = (bf16[2,512,256]{2,1,0:T(8,128)(2,1)S(1)}, bf16[2,512,256]{2,1,0:T(8,128)(2,1)S(1)}, u32[]{:S(2)}, u32[]{:S(2)}) collective-permute-start(bf16[2,512,256]{2,1,0:T(8,128)(2,1)S(1)} %get-tuple-element.24), channel_id=1, source_target_pairs={{1,0},{2,1},{3,2},{4,3},{5,4},{6,5},{7,6},{8,7},{9,8},{10,9},{11,1... | collective-permute-start | bytes 1572872 | tf_op jit(solution)/shard_map/ppermute | solution.py:19
  54.4 1.0 copy-start.4
  54.4 1.3 copy-start.6
  55.7 1.0 copy-start.16
  61.2 3.6 %copy-start.9 = (bf16[10,512,256]{2,1,0:T(8,128)(2,1)}, bf16[10,512,256]{2,1,0:T(8,128)(2,1)S(1)}, u32[]{:S(2)}) copy-start(bf16[10,512,256]{2,1,0:T(8,128)(2,1)S(1)} %get-tuple-element.31) | copy-start | bytes 7864324
  101.3 4.3 %copy-start.5 = (bf16[12,512,80]{1,2,0:T(8,128)(2,1)S(1)}, bf16[12,512,80]{1,2,0:T(8,128)(2,1)}, u32[]{:S(2)}) copy-start(bf16[12,512,80]{1,2,0:T(8,128)(2,1)} %copy-done.4) | copy-start | bytes 2949124
  101.3 4.3 %copy-start.7 = (bf16[12,512,80]{1,2,0:T(8,128)(2,1)S(1)}, bf16[12,512,80]{1,2,0:T(8,128)(2,1)}, u32[]{:S(2)}) copy-start(bf16[12,512,80]{1,2,0:T(8,128)(2,1)} %copy-done.6) | copy-start | bytes 2949124
  101.3 4.3 %copy-start.17 = (bf16[10,512,256]{2,1,0:T(8,128)(2,1)S(1)}, bf16[10,512,256]{2,1,0:T(8,128)(2,1)}, u32[]{:S(2)}) copy-start(bf16[10,512,256]{2,1,0:T(8,128)(2,1)} %get-tuple-element.10) | copy-start | bytes 7864324
  108.2 1.8 %copy-start.10 = (bf16[10,512,256]{2,1,0:T(8,128)(2,1)S(1)}, bf16[10,512,256]{2,1,0:T(8,128)(2,1)}, u32[]{:S(2)}) copy-start(bf16[10,512,256]{2,1,0:T(8,128)(2,1)} %copy-done.9) | copy-start | bytes 7864324
  108.2 2.6 %copy-start.11 = (bf16[10,512,256]{2,1,0:T(8,128)(2,1)S(1)}, bf16[10,512,256]{2,1,0:T(8,128)(2,1)}, u32[]{:S(2)}) copy-start(bf16[10,512,256]{2,1,0:T(8,128)(2,1)} %get-tuple-element.21) | copy-start | bytes 7864324
  108.2 3.4 %copy-start.12 = (bf16[10,512,256]{2,1,0:T(8,128)(2,1)S(1)}, bf16[10,512,256]{2,1,0:T(8,128)(2,1)}, u32[]{:S(2)}) copy-start(bf16[10,512,256]{2,1,0:T(8,128)(2,1)} %get-tuple-element.22) | copy-start | bytes 7864324
  171.5 3.1 %copy-start.15 = (bf16[80,32,128]{2,1,0:T(8,128)(2,1)S(1)}, bf16[80,32,128]{2,1,0:T(8,128)(2,1)}, u32[]{:S(2)}) copy-start(bf16[80,32,128]{2,1,0:T(8,128)(2,1)} %get-tuple-element.13) | copy-start | bytes 1966084
  171.5 3.9 %copy-start.14 = (f32[720,256]{1,0:T(8,128)S(1)}, f32[720,256]{1,0:T(8,128)}, u32[]{:S(2)}) copy-start(f32[720,256]{1,0:T(8,128)} %get-tuple-element.14) | copy-start | bytes 2211844
  171.5 4.7 %copy-start.13 = (f32[2304,256]{1,0:T(8,128)S(1)}, f32[2304,256]{1,0:T(8,128)}, u32[]{:S(2)}) copy-start(f32[2304,256]{1,0:T(8,128)} %get-tuple-element.15) | copy-start | bytes 7077892
  175.4 2.3 %copy-start.1 = (s32[8,128]{1,0:T(8,128)S(1)}, s32[8,128]{1,0:T(8,128)}, u32[]{:S(2)}) copy-start(s32[8,128]{1,0:T(8,128)} %param.11) | copy-start | bytes 12292
